TPU v7x, 32 devices: a 4x4x1 block of a 4x4x8 slice. The times are simulated.
32 devices in a mesh: dp: 1 (over z), col: 4 (over y), row: 8 (over x, core).
Axes of the slice: x: 4, y: 4, z: 1, core: 2. Of those that a mesh axis runs over, the one named last changes fastest.
The devices are a block of a 4x4x8 slice.
Arguments:
- hidden: bfloat16 [128, 2048], P('dp', 'row')
- cache_len: int32 [128], P('dp')
- k_cache: bfloat16 [2, 128, 32, 512, 64], P(None, 'dp', ('col', 'row'))
- v_cache: bfloat16 [2, 128, 32, 512, 64], P(None, 'dp', ('col', 'row'))
- ln1_g: bfloat16 [2, 2048], P(None, 'row')
- ln1_b: bfloat16 [2, 2048], P(None, 'row')
- w_q: bfloat16 [2, 2048, 2048], P(None, 'row', 'col')
- b_q: bfloat16 [2, 2048], P(None, 'col')
- w_k: bfloat16 [2, 2048, 2048], P(None, 'row', 'col')
- b_k: bfloat16 [2, 2048], P(None, 'col')
- w_v: bfloat16 [2, 2048, 2048], P(None, 'row', 'col')
- b_v: bfloat16 [2, 2048], P(None, 'col')
- w_o: bfloat16 [2, 2048, 2048], P(None, 'col', 'row')
- b_o: bfloat16 [2, 2048], P(None, 'row')
- ln2_g: bfloat16 [2, 2048], P(None, 'row')
- ln2_b: bfloat16 [2, 2048], P(None, 'row')
- w_fc1: bfloat16 [2, 2048, 8192], P(None, 'row', 'col')
- b_fc1: bfloat16 [2, 8192], P(None, 'col')
- w_fc2: bfloat16 [2, 8192, 2048], P(None, 'col', 'row')
- b_fc2: bfloat16 [2, 2048], P(None, 'row')
Outputs:
- output 1: bfloat16 [128, 2048], P('dp', 'row')
- output 2: bfloat16 [2, 128, 32, 64], P(None, 'dp', ('col', 'row'))
- output 3: bfloat16 [2, 128, 32, 64], P(None, 'dp', ('col', 'row'))
All inputs are finite; a program needn't handle non-finite values.
Results may differ from a plain program's by a relative error of at most 0.019851.
Values are sent between devices in bfloat16 or wider.
A program may use at most 768 MiB of HBM per device.

v0:
```python
import jax
import jax.numpy as jnp
from jax import lax
from jax.sharding import PartitionSpec as P

EPS_LN = 1e-5


def attention(q_heads, k_fresh, v_fresh, k_layer, v_layer, lengths):
    scores = jnp.einsum("bhd,bhsd->bhs", q_heads, k_layer, preferred_element_type=jnp.float32)
    positions = jnp.arange(k_layer.shape[2])
    scores = jnp.where(positions[None, None, :] < lengths[:, None, None], scores, -jnp.inf)
    score_new = jnp.einsum("bhd,bhd->bh", q_heads, k_fresh, preferred_element_type=jnp.float32)
    peak = jnp.maximum(jnp.max(scores, axis=-1), score_new)
    exp_cache = jnp.exp(scores - peak[:, :, None])
    exp_new = jnp.exp(score_new - peak)
    total_mass = jnp.sum(exp_cache, axis=-1) + exp_new
    prob_cache = (exp_cache / total_mass[:, :, None]).astype(jnp.bfloat16)
    prob_new = (exp_new / total_mass).astype(jnp.bfloat16)
    mixed = jnp.einsum("bhs,bhsd->bhd", prob_cache, v_layer, preferred_element_type=jnp.float32)
    mixed = mixed + prob_new.astype(jnp.float32)[:, :, None] * v_fresh.astype(jnp.float32)
    return mixed.astype(jnp.bfloat16)


def solution(mesh):
    n_row = mesh.shape["row"]
    act_spec = P("dp", "row")
    cache_spec = P(None, "dp", ("col", "row"), None, None)
    fresh_spec = P(None, "dp", ("col", "row"), None)
    in_weight = P(None, "row", "col")
    out_weight = P(None, "col", "row")
    col_vec = P(None, "col")
    row_vec = P(None, "row")
    in_specs = (act_spec, P("dp"), cache_spec, cache_spec, row_vec, row_vec,
                in_weight, col_vec, in_weight, col_vec, in_weight, col_vec,
                out_weight, row_vec, row_vec, row_vec, in_weight, col_vec, out_weight, row_vec)

    def layer_norm(state, gain, shift):
        state_f32 = state.astype(jnp.float32)
        stats = jnp.stack([jnp.sum(state_f32, axis=-1), jnp.sum(state_f32 * state_f32, axis=-1)], axis=-1)
        stats = lax.psum(stats, "row")
        width = state.shape[-1] * n_row
        mean_val = stats[:, 0:1] / width
        variance = stats[:, 1:2] / width - mean_val * mean_val
        normed = (state_f32 - mean_val) * lax.rsqrt(variance + EPS_LN) * gain.astype(jnp.float32) + shift.astype(jnp.float32)
        return normed.astype(jnp.bfloat16)

    def head_projection(normed, weight, bias, scale):
        partial = jnp.dot(normed, weight, preferred_element_type=jnp.float32).astype(jnp.bfloat16)
        summed = lax.psum_scatter(partial, "row", scatter_dimension=1, tiled=True)
        width = summed.shape[1]
        bias_own = lax.dynamic_slice_in_dim(bias, lax.axis_index("row") * width, width)
        return ((summed.astype(jnp.float32) + bias_own.astype(jnp.float32)) * scale).astype(jnp.bfloat16)

    def local_step(hidden, cache_len, k_cache, v_cache, ln1_g, ln1_b, w_q, b_q, w_k, b_k, w_v, b_v,
                   w_o, b_o, ln2_g, ln2_b, w_fc1, b_fc1, w_fc2, b_fc2):
        batch_rows = hidden.shape[0]
        heads_dev = k_cache.shape[2]
        head_dim = k_cache.shape[4]
        scale = head_dim ** -0.5
        state = hidden
        k_rows = []
        v_rows = []
        for layer in range(w_q.shape[0]):
            normed = layer_norm(state, ln1_g[layer], ln1_b[layer])
            q_heads = head_projection(normed, w_q[layer], b_q[layer], scale).reshape(batch_rows, heads_dev, head_dim)
            k_fresh = head_projection(normed, w_k[layer], b_k[layer], 1.0).reshape(batch_rows, heads_dev, head_dim)
            v_fresh = head_projection(normed, w_v[layer], b_v[layer], 1.0).reshape(batch_rows, heads_dev, head_dim)
            attended = attention(q_heads, k_fresh, v_fresh, k_cache[layer], v_cache[layer], cache_len)
            gathered = lax.all_gather(attended.reshape(batch_rows, heads_dev * head_dim), "row", axis=1, tiled=True)
            proj_part = jnp.dot(gathered, w_o[layer], preferred_element_type=jnp.float32).astype(jnp.bfloat16)
            projected = lax.psum(proj_part, "col")
            state_mid = (state.astype(jnp.float32) + (projected.astype(jnp.float32) + b_o[layer].astype(jnp.float32))).astype(jnp.bfloat16)
            normed_two = layer_norm(state_mid, ln2_g[layer], ln2_b[layer])
            inner_part = jnp.dot(normed_two, w_fc1[layer], preferred_element_type=jnp.float32).astype(jnp.bfloat16)
            inner_sum = lax.psum(inner_part, "row")
            inner = jnp.maximum((inner_sum.astype(jnp.float32) + b_fc1[layer].astype(jnp.float32)).astype(jnp.bfloat16), 0)
            out_part = jnp.dot(inner, w_fc2[layer], preferred_element_type=jnp.float32).astype(jnp.bfloat16)
            out_sum = lax.psum(out_part, "col")
            state = (state_mid.astype(jnp.float32) + (out_sum.astype(jnp.float32) + b_fc2[layer].astype(jnp.float32))).astype(jnp.bfloat16)
            k_rows.append(k_fresh)
            v_rows.append(v_fresh)
        return state, jnp.stack(k_rows), jnp.stack(v_rows)

    return jax.shard_map(local_step, mesh=mesh, in_specs=in_specs,
                         out_specs=(act_spec, fresh_spec, fresh_spec), check_vma=False)
```

profile of v0, /device:TPU:97, one launch (start us, length us, event | category | flops | bytes accessed | tf_op | source)
XLA Modules:
  0.0 554.9 jit_solution(17623871941385366333)
XLA Ops:
  8.2 13.9 %psum.70 = f32[128,2]{0,1:T(2,128)S(1)} all-reduce(f32[128,2]{0,1:T(2,128)S(1)} %pad_maximum_fusion.2), channel_id=1, replica_groups=mesh['dp'=1,'col'=4,'row'=8] {'row'}, use_global_device_ids=true, to_apply=%region_2.0 | all-reduce | flops 256 | bytes 2048 | tf_op jit(solution)/shard_map/psum | solution.py:41
  33.9 19.7 %reduce-scatter.9.cloned.1.call-done = bf16[128,64]{0,1:T(8,128)(2,1)} async-done(((bf16[128,512]{0,1:T(8,128)(2,1)}), bf16[128,64]{0,1:T(8,128)(2,1)}) %reduce-scatter.9.cloned.1.call-update) | async-done | bytes 16400 | tf_op jit(solution)/shard_map/reduce_scatter | solution.py:50
  53.6 29.2 %reduce-scatter.7.cloned.1.call-done = bf16[128,64]{0,1:T(8,128)(2,1)} async-done(((bf16[128,512]{0,1:T(8,128)(2,1)}), bf16[128,64]{0,1:T(8,128)(2,1)}) %reduce-scatter.7.cloned.1.call-update) | async-done | bytes 16400 | tf_op jit(solution)/shard_map/reduce_scatter | solution.py:50
  83.9 4.7 fusion.6
  89.2 5.6 %fusion.4 = f32[128,1,64]{2,1,0:T(1,128)S(1)} fusion(bf16[2,128,1,512,64]{3,4,2,1,0:T(8,128)(2,1)} %param.23, bf16[128,512,1]{1,0,2:T(8,128)(2,1)S(1)} %fusion.74), kind=kOutput, calls=%fused_computation.4 | convolution fusion | flops 8388608 | bytes 8552448 | tf_op jit(solution)/shard_map/bhs,bhsd->bhd/dot_general | solution.py:20
  94.9 17.2 %reduce-scatter.11.cloned.1.call-done = bf16[128,64]{0,1:T(8,128)(2,1)} async-done(((bf16[128,512]{0,1:T(8,128)(2,1)}), bf16[128,64]{0,1:T(8,128)(2,1)}) %reduce-scatter.11.cloned.1.call-update) | async-done | bytes 16400 | tf_op jit(solution)/shard_map/reduce_scatter | solution.py:50
  112.9 18.8 %all_gather.6 = bf16[128,512]{0,1:T(8,128)(2,1)S(1)} all-gather(bf16[128,64]{0,1:T(8,128)(2,1)S(1)} %get-tuple-element.15), channel_id=1, replica_groups=mesh['dp'=1,'col'=4,'row'=8] {'row'}, dimensions={1}, use_global_device_ids=true | all-gather | bytes 147456 | tf_op jit(solution)/shard_map/all_gather | solution.py:70
  132.8 40.2 %all-reduce.7.cloned.1.call-done = bf16[128,256]{1,0:T(8,128)(2,1)} async-done(((bf16[128,256]{1,0:T(8,128)(2,1)}), bf16[128,256]{1,0:T(8,128)(2,1)}) %all-reduce.7.cloned.1.call-update) | async-done | bytes 65552 | tf_op jit(solution)/shard_map/psum | solution.py:72
  173.9 14.5 %psum.72 = f32[128,2]{0,1:T(2,128)S(1)} all-reduce(f32[128,2]{0,1:T(2,128)S(1)} %pad_maximum_fusion.3), channel_id=1, replica_groups=mesh['dp'=1,'col'=4,'row'=8] {'row'}, use_global_device_ids=true, to_apply=%region_11.12 | all-reduce | flops 256 | bytes 2048 | tf_op jit(solution)/shard_map/psum | solution.py:41
  189.8 52.0 %all-reduce.9.cloned.1.call-done = bf16[128,2048]{1,0:T(8,128)(2,1)} async-done(((bf16[128,2048]{1,0:T(8,128)(2,1)}), bf16[128,2048]{1,0:T(8,128)(2,1)}) %all-reduce.9.cloned.1.call-update) | async-done | bytes 524304 | tf_op jit(solution)/shard_map/psum | solution.py:76
  241.8 2.3 convolution_convert_fusion.10
  244.3 35.7 %all-reduce.11.cloned.1.call-done = bf16[128,256]{1,0:T(8,128)(2,1)} async-done(((bf16[128,256]{1,0:T(8,128)(2,1)}), bf16[128,256]{1,0:T(8,128)(2,1)}) %all-reduce.11.cloned.1.call-update) | async-done | bytes 65552 | tf_op jit(solution)/shard_map/psum | solution.py:79
  280.9 14.5 %psum.75 = f32[128,2]{0,1:T(2,128)S(1)} all-reduce(f32[128,2]{0,1:T(2,128)S(1)} %pad_maximum_fusion.4), channel_id=1, replica_groups=mesh['dp'=1,'col'=4,'row'=8] {'row'}, use_global_device_ids=true, to_apply=%region_16.17 | all-reduce | flops 256 | bytes 2048 | tf_op jit(solution)/shard_map/psum | solution.py:41
  300.9 19.5 %reduce-scatter.15.cloned.1.call-done = bf16[128,64]{0,1:T(8,128)(2,1)} async-done(((bf16[128,512]{0,1:T(8,128)(2,1)}), bf16[128,64]{0,1:T(8,128)(2,1)}) %reduce-scatter.15.cloned.1.call-update) | async-done | bytes 16400 | tf_op jit(solution)/shard_map/reduce_scatter | solution.py:50
  320.3 29.3 %reduce-scatter.13.cloned.1.call-done = bf16[128,64]{0,1:T(8,128)(2,1)} async-done(((bf16[128,512]{0,1:T(8,128)(2,1)}), bf16[128,64]{0,1:T(8,128)(2,1)}) %reduce-scatter.13.cloned.1.call-update) | async-done | bytes 16400 | tf_op jit(solution)/shard_map/reduce_scatter | solution.py:50
  350.6 4.6 fusion.2
  355.8 5.6 %fusion = f32[128,1,64]{2,1,0:T(1,128)S(1)} fusion(bf16[2,128,1,512,64]{3,4,2,1,0:T(8,128)(2,1)} %param.23, bf16[128,512,1]{1,0,2:T(8,128)(2,1)S(1)} %fusion.75), kind=kOutput, calls=%fused_computation | convolution fusion | flops 8388608 | bytes 8552448 | tf_op jit(solution)/shard_map/bhs,bhsd->bhd/dot_general | solution.py:20
  361.5 17.4 %reduce-scatter.17.cloned.1.call-done = bf16[128,64]{0,1:T(8,128)(2,1)} async-done(((bf16[128,512]{0,1:T(8,128)(2,1)}), bf16[128,64]{0,1:T(8,128)(2,1)}) %reduce-scatter.17.cloned.1.call-update) | async-done | bytes 16400 | tf_op jit(solution)/shard_map/reduce_scatter | solution.py:50
  379.7 18.8 %all_gather.7 = bf16[128,512]{0,1:T(8,128)(2,1)S(1)} all-gather(bf16[128,64]{0,1:T(8,128)(2,1)S(1)} %get-tuple-element.17), channel_id=1, replica_groups=mesh['dp'=1,'col'=4,'row'=8] {'row'}, dimensions={1}, use_global_device_ids=true | all-gather | bytes 147456 | tf_op jit(solution)/shard_map/all_gather | solution.py:70
  399.4 40.1 %all-reduce.13.cloned.1.call-done = bf16[128,256]{1,0:T(8,128)(2,1)} async-done(((bf16[128,256]{1,0:T(8,128)(2,1)}), bf16[128,256]{1,0:T(8,128)(2,1)}) %all-reduce.13.cloned.1.call-update) | async-done | bytes 65552 | tf_op jit(solution)/shard_map/psum | solution.py:72
  440.6 14.5 %psum.77 = f32[128,2]{0,1:T(2,128)S(1)} all-reduce(f32[128,2]{0,1:T(2,128)S(1)} %pad_maximum_fusion.5), channel_id=1, replica_groups=mesh['dp'=1,'col'=4,'row'=8] {'row'}, use_global_device_ids=true, to_apply=%region_25.26 | all-reduce | flops 256 | bytes 2048 | tf_op jit(solution)/shard_map/psum | solution.py:41
  457.0 51.4 %all-reduce.15.cloned.1.call-done = bf16[128,2048]{1,0:T(8,128)(2,1)} async-done(((bf16[128,2048]{1,0:T(8,128)(2,1)}), bf16[128,2048]{1,0:T(8,128)(2,1)}) %all-reduce.15.cloned.1.call-update) | async-done | bytes 524304 | tf_op jit(solution)/shard_map/psum | solution.py:76
  508.3 2.3 convolution_convert_fusion.8
  511.4 35.2 %all-reduce.17.cloned.1.call-done = bf16[128,256]{1,0:T(8,128)(2,1)} async-done(((bf16[128,256]{1,0:T(8,128)(2,1)}), bf16[128,256]{1,0:T(8,128)(2,1)}) %all-reduce.17.cloned.1.call-update) | async-done | bytes 65552 | tf_op jit(solution)/shard_map/psum | solution.py:79
  (97 shorter events, 33.4 us)
Async XLA Ops:
  7.2 81.4 %copy-start.4 = (s32[128]{0:T(128)S(1)}, s32[128]{0:T(128)}, u32[]{:S(2)}) copy-start(s32[128]{0:T(128)} %param.21) | copy-start | bytes 1540
  7.2 46.5 %reduce-scatter.9.cloned.1.call-start = ((), (), s32[]{:S(2)}) async-start(), calls=%async_computation.7 | async-start | bytes 147456 | tf_op jit(solution)/shard_map/reduce_scatter | solution.py:50
  25.6 57.2 %reduce-scatter.7.cloned.1.call-start = ((), (), s32[]{:S(2)}) async-start(), calls=%async_computation.6 | async-start | bytes 147456 | tf_op jit(solution)/shard_map/reduce_scatter | solution.py:50
  27.8 84.4 %reduce-scatter.11.cloned.1.call-start = ((), (), s32[]{:S(2)}) async-start(), calls=%async_computation.8 | async-start | bytes 147456 | tf_op jit(solution)/shard_map/reduce_scatter | solution.py:50
  29.9 143.1 %all-reduce.7.cloned.1.call-start = ((), (), s32[]{:S(2)}) async-start(), calls=%async_computation.9 | async-start | bytes 131072 | tf_op jit(solution)/shard_map/psum | solution.py:72
  83.8 47.9 %copy-start.1 = (bf16[2,512,256]{2,1,0:T(8,128)(2,1)S(1)}, bf16[2,512,256]{2,1,0:T(8,128)(2,1)}, u32[]{:S(2)}) copy-start(bf16[2,512,256]{2,1,0:T(8,128)(2,1)} %param.32) | copy-start | bytes 1572868
  83.8 48.9 %copy-start.5 = (bf16[2,256]{1,0:T(2,128)(2,1)S(1)}, bf16[2,256]{1,0:T(2,128)(2,1)}, u32[]{:S(2)}) copy-start(bf16[2,256]{1,0:T(2,128)(2,1)} %param.35) | copy-start | bytes 3076
  83.9 89.1 %copy-start.2 = (bf16[128,256]{1,0:T(8,128)(2,1)S(1)}, bf16[128,256]{1,0:T(8,128)(2,1)}, u32[]{:S(2)}) copy-start(bf16[128,256]{1,0:T(8,128)(2,1)} %param.20) | copy-start | bytes 196612
  83.9 104.5 %copy-start = (bf16[2,256,2048]{2,1,0:T(8,128)(2,1)S(1)}, bf16[2,256,2048]{2,1,0:T(8,128)(2,1)}, u32[]{:S(2)}) copy-start(bf16[2,256,2048]{2,1,0:T(8,128)(2,1)} %param.36) | copy-start | bytes 6291460
  88.6 101.1 %copy-start.3 = (bf16[2,2048]{1,0:T(2,128)(2,1)S(1)}, bf16[2,2048]{1,0:T(2,128)(2,1)}, u32[]{:S(2)}) copy-start(bf16[2,2048]{1,0:T(2,128)(2,1)} %param.37) | copy-start | bytes 24580
  88.6 155.7 %copy-start.6 = (bf16[2,256]{1,0:T(2,128)(2,1)S(1)}, bf16[2,256]{1,0:T(2,128)(2,1)}, u32[]{:S(2)}) copy-start(bf16[2,256]{1,0:T(2,128)(2,1)} %param.39) | copy-start | bytes 3076
  88.6 206.8 %copy-start.7 = (bf16[2,256,512]{2,1,0:T(8,128)(2,1)S(1)}, bf16[2,256,512]{2,1,0:T(8,128)(2,1)}, u32[]{:S(2)}) copy-start(bf16[2,256,512]{2,1,0:T(8,128)(2,1)} %param.28) | copy-start | bytes 1572868
  132.7 109.1 %all-reduce.9.cloned.1.call-start = ((), (), s32[]{:S(2)}) async-start(), calls=%async_computation.10 | async-start | bytes 1048576 | tf_op jit(solution)/shard_map/psum | solution.py:76
  189.7 90.3 %all-reduce.11.cloned.1.call-start = ((), (), s32[]{:S(2)}) async-start(), calls=%async_computation.11 | async-start | bytes 131072 | tf_op jit(solution)/shard_map/psum | solution.py:79
  244.2 76.2 %reduce-scatter.15.cloned.1.call-start = ((), (), s32[]{:S(2)}) async-start(), calls=%async_computation.13 | async-start | bytes 147456 | tf_op jit(solution)/shard_map/reduce_scatter | solution.py:50
  296.5 53.1 %reduce-scatter.13.cloned.1.call-start = ((), (), s32[]{:S(2)}) async-start(), calls=%async_computation.12 | async-start | bytes 147456 | tf_op jit(solution)/shard_map/reduce_scatter | solution.py:50
  298.6 80.2 %reduce-scatter.17.cloned.1.call-start = ((), (), s32[]{:S(2)}) async-start(), calls=%async_computation.14 | async-start | bytes 147456 | tf_op jit(solution)/shard_map/reduce_scatter | solution.py:50
  300.8 138.8 %all-reduce.13.cloned.1.call-start = ((), (), s32[]{:S(2)}) async-start(), calls=%async_computation.15 | async-start | bytes 131072 | tf_op jit(solution)/shard_map/psum | solution.py:72
  399.4 109.0 %all-reduce.15.cloned.1.call-start = ((), (), s32[]{:S(2)}) async-start(), calls=%async_computation.16 | async-start | bytes 1048576 | tf_op jit(solution)/shard_map/psum | solution.py:76
  456.3 90.2 %all-reduce.17.cloned.1.call-start = ((), (), s32[]{:S(2)}) async-start(), calls=%async_computation.17 | async-start | bytes 131072 | tf_op jit(solution)/shard_map/psum | solution.py:79
Sparse Core Ops, SparseCore 0:
  25.8 27.8 reduce-scatter.8
  55.9 26.9 reduce-scatter.6
  85.1 26.9 reduce-scatter.10
  132.8 40.1 all-reduce.6
  189.8 51.9 all-reduce.8
  244.6 35.3 all-reduce.10
  296.6 23.6 reduce-scatter.14
  322.6 26.9 reduce-scatter.12
  351.9 26.9 reduce-scatter.16
  399.5 40.0 all-reduce.12
  456.4 51.8 all-reduce.14
  511.1 35.3 all-reduce.16
where the time goes:
time: 557 us; the launch traced here: 555 us
  waiting for transfers between devices  388 us (70%)
  blocking collectives  94.9 us (17%)
  matrix products  40.1 us (7%)
  between operations  14.5 us (3%)
  other arithmetic  14.4 us (3%)
    reduce_scatter x6, waiting for transfers between devices, head_projection(): summed = lax.psum_scatter(partial, 'row', scatter_dimension=1, tiled=True)  132 us
    psum x2, waiting for transfers between devices, local_step(): inner_sum = lax.psum(inner_part, 'row')  103 us
    psum x2, waiting for transfers between devices, local_step(): projected = lax.psum(proj_part, 'col')  80.3 us
    psum x2, waiting for transfers between devices, local_step(): out_sum = lax.psum(out_part, 'col')  70.8 us
    psum x4, blocking collectives, layer_norm(): stats = lax.psum(stats, 'row')  57.3 us
    all_gather x2, blocking collectives, local_step(): lax.all_gather(attended.reshape(batch_rows, heads_dev * head_dim), 'row',...  37.6 us
    dot_general x2, matrix products, attention(): jnp.einsum('bhs,bhsd->bhd', prob_cache, v_layer, preferred_element_type=j...  11.3 us
  transfers between devices with their start and end apart: 12, of which 12 were waited for; matrix products, arithmetic and copies ran while one was open for 7% of the time, Pallas kernels for 0%

commit v1 on v0

v1 whole, which is shorter than its diff:
```python
import functools

import jax
import jax.numpy as jnp
from jax import lax
from jax.experimental import pallas as pl
from jax.experimental.pallas import tpu as pltpu
from jax.sharding import PartitionSpec as P

EPS_LN = 1e-5
F32 = jnp.float32
BF16 = jnp.bfloat16
MESH = pl.DeviceIdType.MESH


def kernel(n_row, n_col, width,
           x_hbm, len_hbm, k_hbm, v_hbm, ln1g_hbm, ln1b_hbm, wq_hbm, bq_hbm, wk_hbm, bk_hbm, wv_hbm, bv_hbm,
           wo_hbm, bo_hbm, ln2g_hbm, ln2b_hbm, w1_hbm, b1_hbm, w2_hbm, b2_hbm,
           h_out, k_out, v_out,
           x_buf, len_buf, k_buf, v_buf, ln1g, ln1b, wq, bq, wk, bk, wv, bv, wo, bo, ln2g, ln2b, w1, b1, w2, b2,
           stat_src, stat_in, qkv_src, qkv_in, att_in, proj_in, up_src, up_in, act_in, down_in,
           state, twin, onehot, scores, probs_t, kt_buf, vt_buf, h_buf,
           in_sem, kv_sem, out_sem, send_sem, stat_sem, qkv_sem, att_sem, proj_sem, up_sem, act_sem, down_sem):
    layers = wq.shape[0]
    rows, cols = x_buf.shape
    head = k_buf.shape[2]
    lanes = 2 * head
    half = rows // 2
    n_chip = n_row // 2
    me = lax.axis_index("row")
    mine = lax.axis_index("col")
    chip = me // 2
    core = lax.rem(me, 2)

    smalls = [(x_hbm, x_buf), (len_hbm, len_buf), (ln1g_hbm, ln1g), (ln1b_hbm, ln1b), (bq_hbm, bq), (bk_hbm, bk),
              (bv_hbm, bv), (bo_hbm, bo), (ln2g_hbm, ln2g), (ln2b_hbm, ln2b), (b1_hbm, b1), (b2_hbm, b2)]
    small_copies = [pltpu.make_async_copy(src, dst, in_sem.at[i]) for i, (src, dst) in enumerate(smalls)]
    base = len(smalls)
    weights = [(wq_hbm, wq), (wk_hbm, wk), (wv_hbm, wv), (wo_hbm, wo), (w1_hbm, w1), (w2_hbm, w2)]
    weight_copies = [[pltpu.make_async_copy(src.at[l], dst.at[l], in_sem.at[base + l * len(weights) + i])
                      for i, (src, dst) in enumerate(weights)] for l in range(layers)]
    steps = rows // 16

    def cache_copy(l, which, t):
        src, dst = ((k_hbm, k_buf), (v_hbm, v_buf))[which]
        return pltpu.make_async_copy(src.at[l, pl.ds(16 * t, 16)], dst.at[l, pl.ds(16 * t, 16)], kv_sem.at[l, which, t])

    for copy in small_copies:
        copy.start()
    for l in range(layers):
        for copy in weight_copies[l][:3]:
            copy.start()
        for which in range(2):
            for t in range(steps):
                cache_copy(l, which, t).start()
        for copy in weight_copies[l][3:]:
            copy.start()

    barrier = pltpu.get_barrier_semaphore()
    for k in range(1, n_row):
        pl.semaphore_signal(barrier, inc=1, device_id={"row": lax.rem(me + k, n_row)}, device_id_type=MESH)
    for k in range(1, n_col):
        pl.semaphore_signal(barrier, inc=1, device_id={"col": lax.rem(mine + k, n_col)}, device_id_type=MESH)

    chip_order = [2, 1, 3] if n_chip == 4 else list(range(1, n_chip))

    def remote(src, dst, ssem, rsem, target):
        copy = pltpu.make_async_remote_copy(src_ref=src, dst_ref=dst, send_sem=ssem, recv_sem=rsem,
                                            device_id=target, device_id_type=MESH)
        copy.start()
        return copy

    def await_recv(dst, sem):
        pltpu.make_async_remote_copy(src_ref=dst, dst_ref=dst, send_sem=sem, recv_sem=sem,
                                     device_id={"row": me}, device_id_type=MESH).wait_recv()

    def row_peers():
        for dc in chip_order:
            for e in range(2):
                yield lax.rem(chip + dc, n_chip) * 2 + lax.rem(core + e, 2)
        yield chip * 2 + (1 - core)

    lane_id = lax.broadcasted_iota(jnp.int32, (16, 16 * head), 1)
    row_id = lax.broadcasted_iota(jnp.int32, (16, 16 * head), 0)
    onehot[...] = jnp.where(lane_id // head == row_id, 1.0, 0.0).astype(BF16)

    for copy in small_copies:
        copy.wait()

    def own_head(vec_ref, l):
        total = jnp.zeros((1, head), F32)
        for j in range(n_row):
            total = total + jnp.where(me == j, vec_ref[l:l + 1, j * head:(j + 1) * head].astype(F32), 0.0)
        return total

    len_col = jnp.transpose(jnp.broadcast_to(len_buf[...], (rows, rows)))[:, 0:1]
    state[...] = x_buf[...]
    pending = []

    def exchange_stats(n):
        xs = state[...].astype(F32)
        s1 = jnp.sum(xs, axis=1, keepdims=True)
        s2 = jnp.sum(xs * xs, axis=1, keepdims=True)
        lane = lax.broadcasted_iota(jnp.int32, (rows, 128), 1)
        both = jnp.where(lane == 0, s1, jnp.where(lane == 1, s2, 0.0))
        stat_src[n] = jnp.transpose(both)[0:8, :]
        if n == 0:
            pl.semaphore_wait(barrier, n_row + n_col - 2)
        for target in row_peers():
            pending.append(remote(stat_src.at[n], stat_in.at[n, me], send_sem.at[0], stat_sem.at[n, me], {"row": target}))
        stat_in[n, me] = stat_src[n]
        for k in range(1, n_row):
            j = lax.rem(me + k, n_row)
            await_recv(stat_in.at[n, j], stat_sem.at[n, j])
        total = stat_in[n, 0]
        for j in range(1, n_row):
            total = total + stat_in[n, j]
        mean = total[0:1, :] / width
        var = total[1:2, :] / width - mean * mean
        inv = lax.rsqrt(var + EPS_LN)
        mean_b = jnp.transpose(jnp.broadcast_to(mean, (128, rows)))
        inv_b = jnp.transpose(jnp.broadcast_to(inv, (128, rows)))
        return mean_b[:, 0:1], inv_b[:, 0:1]

    def layer_norm(n, gain, shift):
        mean, inv = exchange_stats(n)
        xs = state[...].astype(F32)
        return ((xs - mean) * inv * gain.astype(F32) + shift.astype(F32)).astype(BF16)

    low = lax.broadcasted_iota(jnp.int32, (rows, lanes), 1) < head
    low_half = low[0:half]

    for l in range(layers):
        normed = layer_norm(2 * l, ln1g[l:l + 1, :], ln1b[l:l + 1, :])
        for copy in weight_copies[l][:3]:
            copy.wait()
        for i, dc in enumerate(chip_order + [0]):
            dest = lax.rem(chip + dc, n_chip)
            at = pl.ds(pl.multiple_of(dest * lanes, lanes), lanes)
            qp = jnp.dot(normed, wq[l, :, at], preferred_element_type=F32)
            kp = jnp.dot(normed, wk[l, :, at], preferred_element_type=F32)
            vp = jnp.dot(normed, wv[l, :, at], preferred_element_type=F32)
            q_r = pltpu.roll(qp, head, axis=1)
            k_r = pltpu.roll(kp, head, axis=1)
            v_r = pltpu.roll(vp, head, axis=1)
            qkv_src[l, i, 0, 0:rows] = jnp.where(low, qp, k_r).astype(BF16)
            qkv_src[l, i, 1, 0:rows] = jnp.where(low, q_r, kp).astype(BF16)
            qkv_src[l, i, 0, rows:] = jnp.where(low_half, vp[0:half], v_r[half:]).astype(BF16)
            qkv_src[l, i, 1, rows:] = jnp.where(low_half, v_r[0:half], vp[half:]).astype(BF16)
            if dc != 0:
                for e in range(2):
                    pending.append(remote(qkv_src.at[l, i, e], qkv_in.at[l, me], send_sem.at[1], qkv_sem.at[l, me],
                                          {"row": dest * 2 + e}))
            else:
                pending.append(remote(qkv_src.at[l, i, 1 - core], qkv_in.at[l, me], send_sem.at[1], qkv_sem.at[l, me],
                                      {"row": dest * 2 + (1 - core)}))
        own = qkv_src[l, n_chip - 1, core]
        qkv_in[l, me] = own
        for k in range(1, n_row):
            j = lax.rem(me + k, n_row)
            await_recv(qkv_in.at[l, j], qkv_sem.at[l, j])
        total = qkv_in[l, 0].astype(F32)
        for j in range(1, n_row):
            total = total + qkv_in[l, j].astype(F32)
        scale = head ** -0.5
        qk = total[0:rows]
        vv = total[rows:]
        q_b = ((qk[:, 0:head] + own_head(bq, l)) * scale).astype(BF16)
        k_new = (pltpu.roll(qk, head, axis=1)[:, 0:head] + own_head(bk, l)).astype(BF16)
        v_new = (jnp.concatenate([vv[:, 0:head], pltpu.roll(vv, head, axis=1)[:, 0:head]], axis=0)
                 + own_head(bv, l)).astype(BF16)
        q_f = q_b.astype(F32)
        k_f = k_new.astype(F32)
        twin[...] = jnp.concatenate([q_f, q_f], axis=1).astype(BF16)
        kt_buf[l] = jnp.transpose(k_f).astype(BF16)
        v_t = jnp.transpose(v_new.astype(F32))
        vt_buf[l] = v_t.astype(BF16)
        pending.append(pltpu.make_async_copy(kt_buf.at[l], k_out.at[l], out_sem.at[0, l]))
        pending[-1].start()
        pending.append(pltpu.make_async_copy(vt_buf.at[l], v_out.at[l], out_sem.at[1, l]))
        pending[-1].start()
        score_new = jnp.sum(q_f * k_f, axis=1, keepdims=True)

        def score_step(t, carry, l=l):
            cache_copy(l, 0, t).wait()
            q_blk = twin[pl.ds(pl.multiple_of(16 * t, 16), 16), :]
            q_diag = jnp.concatenate([q_blk] * (16 * head // lanes), axis=1) * onehot[...]
            keys = k_buf[l, pl.ds(16 * t, 16)].reshape(16 * head, k_buf.shape[3])
            scores[pl.ds(pl.multiple_of(16 * t, 16), 16), :] = jnp.dot(q_diag, keys, preferred_element_type=F32)
            return carry

        lax.fori_loop(0, steps, score_step, 0)
        sc = scores[...]
        position = lax.broadcasted_iota(jnp.int32, sc.shape, 1)
        sc = jnp.where(position < len_col, sc, -jnp.inf)
        peak = jnp.maximum(jnp.max(sc, axis=1, keepdims=True), score_new)
        ex = jnp.exp(sc - peak)
        ex_new = jnp.exp(score_new - peak)
        mass = jnp.sum(ex, axis=1, keepdims=True) + ex_new
        scores[...] = ex / mass
        prob_new = (ex_new / mass).astype(BF16).astype(F32)
        for b in range(k_buf.shape[3] // 128):
            probs_t[b * 128:(b + 1) * 128, :] = jnp.transpose(scores[:, b * 128:(b + 1) * 128]).astype(BF16)
        prob_row = jnp.transpose(jnp.broadcast_to(prob_new, (rows, 128)))[0:1, :]
        lane64 = lax.broadcasted_iota(jnp.int32, (head, rows), 1)

        def mix_step(t, acc, l=l):
            cache_copy(l, 1, t).wait()
            values = v_buf[l, pl.ds(16 * t, 16)].reshape(16 * head, v_buf.shape[3])
            full = jnp.dot(values, probs_t[...], preferred_element_type=F32)
            for i in range(16):
                acc = jnp.where(lane64 == 16 * t + i, full[i * head:(i + 1) * head], acc)
            return acc

        mixed = lax.fori_loop(0, steps, mix_step, jnp.zeros((head, rows), F32))
        mixed = mixed + prob_row * v_t
        att_in[l, me] = mixed.astype(BF16)
        for target in row_peers():
            pending.append(remote(att_in.at[l, me], att_in.at[l, me], send_sem.at[2], att_sem.at[l, me], {"row": target}))
        weight_copies[l][3].wait()
        for k in range(1, n_row):
            j = lax.rem(me + k, n_row)
            await_recv(att_in.at[l, j], att_sem.at[l, j])
        gathered = att_in[l].reshape(n_row * head, rows)
        part = lax.dot_general(gathered, wo[l], (((0,), (0,)), ((), ())), preferred_element_type=F32)
        proj_in[l, mine] = part.astype(BF16)

        def all_reduce_col(buf, sem, bias, base_state):
            for k in (2, 1, 3) if n_col == 4 else range(1, n_col):
                pending.append(remote(buf.at[l, mine], buf.at[l, mine], send_sem.at[3], sem.at[l, mine],
                                      {"col": lax.rem(mine + k, n_col)}))
            for k in range(1, n_col):
                j = lax.rem(mine + k, n_col)
                await_recv(buf.at[l, j], sem.at[l, j])
            summed = buf[l, 0].astype(F32)
            for j in range(1, n_col):
                summed = summed + buf[l, j].astype(F32)
            return (base_state.astype(F32) + (summed + bias.astype(F32))).astype(BF16)

        state[...] = all_reduce_col(proj_in, proj_sem, bo[l:l + 1, :], state[...])
        normed = layer_norm(2 * l + 1, ln2g[l:l + 1, :], ln2b[l:l + 1, :])
        weight_copies[l][4].wait()
        for i, target in enumerate(row_peers()):
            at = pl.ds(pl.multiple_of(target * cols, cols), cols)
            up_src[l, i] = jnp.dot(normed, w1[l, :, at], preferred_element_type=F32).astype(BF16)
            pending.append(remote(up_src.at[l, i], up_in.at[l, me], send_sem.at[4], up_sem.at[l, me], {"row": target}))
        own_at = pl.ds(pl.multiple_of(me * cols, cols), cols)
        up_in[l, me] = jnp.dot(normed, w1[l, :, own_at], preferred_element_type=F32).astype(BF16)
        for k in range(1, n_row):
            j = lax.rem(me + k, n_row)
            await_recv(up_in.at[l, j], up_sem.at[l, j])
        summed = up_in[l, 0].astype(F32)
        for j in range(1, n_row):
            summed = summed + up_in[l, j].astype(F32)
        inner = jnp.maximum((summed + b1[l:l + 1, own_at].astype(F32)).astype(BF16), 0)
        act_in[l, me] = inner
        for target in row_peers():
            pending.append(remote(act_in.at[l, me], act_in.at[l, me], send_sem.at[5], act_sem.at[l, me], {"row": target}))
        weight_copies[l][5].wait()
        for k in range(1, n_row):
            j = lax.rem(me + k, n_row)
            await_recv(act_in.at[l, j], act_sem.at[l, j])
        part = jnp.dot(act_in[l, 0], w2[l, 0:cols, :], preferred_element_type=F32)
        for j in range(1, n_row):
            part = part + jnp.dot(act_in[l, j], w2[l, j * cols:(j + 1) * cols, :], preferred_element_type=F32)
        down_in[l, mine] = part.astype(BF16)
        state[...] = all_reduce_col(down_in, down_sem, b2[l:l + 1, :], state[...])

    h_buf[...] = state[...]
    last = pltpu.make_async_copy(h_buf, h_out, out_sem.at[0, 0])
    for copy in pending:
        if not copy.is_remote:
            copy.wait()
        else:
            copy.wait_send()
    last.start()
    last.wait()


def solution(mesh):
    n_row = mesh.shape["row"]
    n_col = mesh.shape["col"]
    act_spec = P("dp", "row")
    cache_spec = P(None, "dp", ("col", "row"), None, None)
    fresh_spec = P(None, "dp", ("col", "row"), None)
    in_weight = P(None, "row", "col")
    out_weight = P(None, "col", "row")
    col_vec = P(None, "col")
    row_vec = P(None, "row")
    in_specs = (act_spec, P("dp"), cache_spec, cache_spec, row_vec, row_vec,
                in_weight, col_vec, in_weight, col_vec, in_weight, col_vec,
                out_weight, row_vec, row_vec, row_vec, in_weight, col_vec, out_weight, row_vec)

    def local_step(hidden, cache_len, k_cache, v_cache, *params):
        rows, cols = hidden.shape
        layers, _, _, s_max, head = k_cache.shape
        keys = jnp.swapaxes(k_cache, 3, 4).reshape(layers, rows, head, s_max)
        values = jnp.swapaxes(v_cache, 3, 4).reshape(layers, rows, head, s_max)
        operands = (hidden, cache_len.reshape(1, rows), keys, values) + params
        vmem = [pltpu.VMEM(a.shape, a.dtype) for a in operands]
        dma = pltpu.SemaphoreType.DMA
        ff = params[12].shape[2]
        scratch = vmem + [
            pltpu.VMEM((2 * layers, 8, rows), F32),
            pltpu.VMEM((2 * layers, n_row, 8, rows), F32),
            pltpu.VMEM((layers, n_row // 2, 2, rows + rows // 2, 2 * head), BF16),
            pltpu.VMEM((layers, n_row, rows + rows // 2, 2 * head), BF16),
            pltpu.VMEM((layers, n_row, head, rows), BF16),
            pltpu.VMEM((layers, n_col, rows, cols), BF16),
            pltpu.VMEM((layers, n_row - 1, rows, ff // n_row), BF16),
            pltpu.VMEM((layers, n_row, rows, ff // n_row), BF16),
            pltpu.VMEM((layers, n_row, rows, ff // n_row), BF16),
            pltpu.VMEM((layers, n_col, rows, cols), BF16),
            pltpu.VMEM((rows, cols), BF16),
            pltpu.VMEM((rows, 2 * head), BF16),
            pltpu.VMEM((16, 16 * head), BF16),
            pltpu.VMEM((rows, s_max), F32),
            pltpu.VMEM((s_max, rows), BF16),
            pltpu.VMEM((layers, head, rows), BF16),
            pltpu.VMEM((layers, head, rows), BF16),
            pltpu.VMEM((rows, cols), BF16),
            dma((12 + 6 * layers,)),
            dma((layers, 2, rows // 16)),
            dma((2, layers)),
            dma((8,)),
            dma((2 * layers, n_row)),
            dma((layers, n_row)),
            dma((layers, n_row)),
            dma((layers, n_col)),
            dma((layers, n_row)),
            dma((layers, n_row)),
            dma((layers, n_col)),
        ]
        h, kt, vt = pl.pallas_call(
            functools.partial(kernel, n_row, n_col, cols * n_row),
            out_shape=(jax.ShapeDtypeStruct((rows, cols), BF16),
                       jax.ShapeDtypeStruct((layers, head, rows), BF16),
                       jax.ShapeDtypeStruct((layers, head, rows), BF16)),
            in_specs=[pl.BlockSpec(memory_space=pltpu.HBM)] * len(operands),
            out_specs=[pl.BlockSpec(memory_space=pltpu.HBM)] * 3,
            scratch_shapes=scratch,
            compiler_params=pltpu.CompilerParams(collective_id=0, has_side_effects=True,
                                                 vmem_limit_bytes=63 * 2 ** 20),
        )(*operands)
        k_new = jnp.swapaxes(kt, 1, 2).reshape(layers, rows, 1, head)
        v_new = jnp.swapaxes(vt, 1, 2).reshape(layers, rows, 1, head)
        return h, k_new, v_new

    return jax.shard_map(local_step, mesh=mesh, in_specs=in_specs,
                         out_specs=(act_spec, fresh_spec, fresh_spec), check_vma=False)
```

time: 557 us -> 122 us (0.22)
  waiting for transfers between devices: 388 us -> 0 us
  Pallas kernels: 0 us -> 117 us
  blocking collectives: 94.9 us -> 0 us
  matrix products: 40.1 us -> 0 us
  other arithmetic: 14.4 us -> 0 us
  between operations: 14.5 us -> 0.65 us
    psum x6 -> x0, waiting for transfers between devices: 255 us -> none  [the longest x2 103 us: local_step(): inner_sum = lax.psum(inner_part, 'row')]
    reduce_scatter x6 -> x0, waiting for transfers between devices: 132 us -> none  [head_projection(): summed = lax.psum_scatter(partial, 'row', scatter_dimension=1, tiled=True)]
    pallas_call x0 -> x1, Pallas kernels: none -> 117 us  [local_step(): pl.pallas_call(functools.partial(kernel, n_row, n_col, cols * n_row), out...]
    psum x4 -> x0, blocking collectives: 57.3 us -> none  [layer_norm(): stats = lax.psum(stats, 'row')]
    dot_general x16 -> x0, matrix products: 40.1 us -> none  [the longest x2 11.3 us: attention(): jnp.einsum('bhs,bhsd->bhd', prob_cache, v_layer, preferred_element_type=j...]
    all_gather x2 -> x0, blocking collectives: 37.6 us -> none  [local_step(): lax.all_gather(attended.reshape(batch_rows, heads_dev * head_dim), 'row',...]
  transfers between devices with their start and end apart: 12 -> 0, of which waited for: 12 -> 0; matrix products, arithmetic and copies ran while one was open for 7% -> 0% of each run, Pallas kernels for 0% -> 0%
where the time goes in v1:
time: 122 us
  Pallas kernels  117 us (96%)
  local copies, waits for them, and re-layouts  4.22 us (3%)
    pallas_call x1, Pallas kernels, local_step(): pl.pallas_call(functools.partial(kernel, n_row, n_col, cols * n_row), out...  117 us
    unnamed x3, local copies, waits for them, and re-layouts  4.22 us

profile of v1, /device:TPU:97, one launch (start us, length us, event | category | flops | bytes accessed | tf_op | source)
XLA Modules:
  0.0 121.6 jit_solution(17094435550307656843)
XLA Ops:
  0.6 116.7 %shard_map.211 = (bf16[128,256]{1,0:T(8,128)(2,1)}, bf16[2,64,128]{2,1,0:T(8,128)(2,1)}, bf16[2,64,128]{2,1,0:T(8,128)(2,1)}) custom-call(bf16[128,256]{1,0:T(8,128)(2,1)} %x_hbm.1, s32[1,128]{1,0:T(1,128)} %bitcast.25, bf16[2,128,64,512]{3,2,1,0:T(8,128)(2,1)} %bitcast.21, bf16[2,128,64,512]{3,2,1,0:T(8,128)(2,1)} %bitcast.22, bf16[2,256]{1,0:T(2,128)(2,1)} %ln1g_hbm.1, ...), custom_call_target="tpu_custom_call" | custom-call | tf_op jit(solution)/shard_map/pallas_call | solution.py:334
  117.3 1.5 %copy.30 = bf16[128,256]{1,0:T(8,128)(2,1)} copy(bf16[128,256]{1,0:T(8,128)(2,1)} %get-tuple-element.15) | data formatting | bytes 131072
  118.8 1.4 %copy.31 = bf16[2,128,1,64]{1,3,2,0:T(8,128)(2,1)} copy(bf16[2,128,1,64]{1,3,2,0:T(8,128)(2,1)} %bitcast.24) | data formatting | bytes 65536
  120.2 1.4 %copy.32 = bf16[2,128,1,64]{1,3,2,0:T(8,128)(2,1)} copy(bf16[2,128,1,64]{1,3,2,0:T(8,128)(2,1)} %bitcast.23) | data formatting | bytes 65536

commit v2 on v0

v2 whole, which is shorter than its diff:
```python
import functools

import jax
import jax.numpy as jnp
from jax import lax
from jax.experimental import pallas as pl
from jax.experimental.pallas import tpu as pltpu
from jax.sharding import PartitionSpec as P

EPS_LN = 1e-5
F32 = jnp.float32
BF16 = jnp.bfloat16
MESH = pl.DeviceIdType.MESH


class Marks:
    def __init__(self):
        self.open = None

    def __call__(self, name):
        if self.open is not None:
            self.open.__exit__(None, None, None)
        self.open = None
        if name:
            self.open = jax.named_scope(name)
            self.open.__enter__()


def kernel(n_row, n_col, width,
           x_hbm, len_hbm, k_hbm, v_hbm, ln1g_hbm, ln1b_hbm, wq_hbm, bq_hbm, wk_hbm, bk_hbm, wv_hbm, bv_hbm,
           wo_hbm, bo_hbm, ln2g_hbm, ln2b_hbm, w1_hbm, b1_hbm, w2_hbm, b2_hbm,
           h_out, k_out, v_out,
           len_buf, k_buf, v_buf, ln1g, ln1b, wq, bq, wk, bk, wv, bv, wo, bo, ln2g, ln2b, w1, b1, w2, b2,
           state, pair, stat_src, stat_in, cq_src, cq_in, cu_src, cu_in,
           qkv_src, qkv_in, att_in, proj_in, up_src, up_in, act_in, down_in,
           twin, onehot, scores, probs_t,
           in_sem, kv_sem, send_sem, pw_sem, pair_sem, stat_sem, cq_sem, cu_sem,
           qkv_sem, att_sem, proj_sem, up_sem, act_sem, down_sem):
    mark = Marks()
    mark("entry")
    layers = wo.shape[0]
    rows, cols = state.shape[1:]
    head = k_buf.shape[2]
    s_max = k_buf.shape[3]
    lanes = 2 * head
    half = rows // 2
    n_chip = n_row // 2
    near = width // n_chip
    ff = w1.shape[3]
    me = lax.axis_index("row")
    mine = lax.axis_index("col")
    chip = me // 2
    core = lax.rem(me, 2)
    partner = chip * 2 + (1 - core)
    hops = [2, 1, 3] if n_chip == 4 else list(range(1, n_chip))
    far = len(hops)
    dests = [lax.rem(chip + dc, n_chip) for dc in hops] + [chip]
    pending = []

    def local(src, dst, sem):
        copy = pltpu.make_async_copy(src, dst, sem)
        copy.start()
        return copy

    def remote(src, dst, ssem, rsem, target):
        copy = pltpu.make_async_remote_copy(src_ref=src, dst_ref=dst, send_sem=ssem, recv_sem=rsem,
                                            device_id=target, device_id_type=MESH)
        copy.start()
        pending.append(copy)

    def await_recv(dst, sem):
        pltpu.make_async_remote_copy(src_ref=dst, dst_ref=dst, send_sem=sem, recv_sem=sem,
                                     device_id={"row": me}, device_id_type=MESH).wait_recv()

    def cache_copy(l, which, t):
        src, dst = ((k_hbm, k_buf), (v_hbm, v_buf))[which]
        return pltpu.make_async_copy(src.at[l, pl.ds(16 * t, 16)], dst.at[l, pl.ds(16 * t, 16)], kv_sem.at[l, which, t])

    steps = rows // 16
    norms = [(ln1g_hbm, ln1g), (ln1b_hbm, ln1b), (ln2g_hbm, ln2g), (ln2b_hbm, ln2b)]
    smalls = ([(x_hbm, state.at[0]), (len_hbm, len_buf), (bq_hbm, bq), (bk_hbm, bk), (bv_hbm, bv), (bo_hbm, bo),
               (b1_hbm, b1), (b2_hbm, b2)] + [(src, dst.at[0]) for src, dst in norms])
    small_copies = [local(src, dst, in_sem.at[0, i]) for i, (src, dst) in enumerate(smalls)]

    barrier = pltpu.get_barrier_semaphore()
    for k in range(1, n_row):
        pl.semaphore_signal(barrier, inc=1, device_id={"row": lax.rem(me + k, n_row)}, device_id_type=MESH)
    for k in range(1, n_col):
        pl.semaphore_signal(barrier, inc=1, device_id={"col": lax.rem(mine + k, n_col)}, device_id_type=MESH)

    def up_columns(i, which):
        return pl.ds(pl.multiple_of((dests[i] * 2 + which) * ff, ff), ff)

    def load_qkv(l):
        return [local(src.at[l], dst.at[l, 0:cols], in_sem.at[1 + l, i])
                for i, (src, dst) in enumerate([(wq_hbm, wq), (wk_hbm, wk), (wv_hbm, wv)])]

    def share_qkv(l):
        for i, (src, dst) in enumerate([(wq_hbm, wq), (wk_hbm, wk), (wv_hbm, wv)]):
            remote(src.at[l], dst.at[l, cols:], send_sem.at[6], pw_sem.at[l, i], {"row": partner})

    def load_rest(l):
        got = [local(wo_hbm.at[l], wo.at[l], in_sem.at[1 + l, 3]), local(w2_hbm.at[l], w2.at[l], in_sem.at[1 + l, 4])]
        return got + [local(w1_hbm.at[l, :, up_columns(i, core)], w1.at[l, i, 0:cols], in_sem.at[1 + l, 5 + i])
                      for i in range(n_chip)]

    def share_up(l):
        for i in range(n_chip):
            remote(w1_hbm.at[l, :, up_columns(i, 1 - core)], w1.at[l, i, cols:], send_sem.at[7], pw_sem.at[l, 3 + i],
                   {"row": partner})

    def load_cache(l):
        for which in range(2):
            for t in range(steps):
                cache_copy(l, which, t).start()

    loads = {("qkv", 0): load_qkv(0)}
    lane_id = lax.broadcasted_iota(jnp.int32, (16, 16 * head), 1)
    row_id = lax.broadcasted_iota(jnp.int32, (16, 16 * head), 0)
    onehot[...] = jnp.where(lane_id // head == row_id, 1.0, 0.0).astype(BF16)
    for copy in small_copies:
        copy.wait()
    mark("barrier")
    pl.semaphore_wait(barrier, n_row + n_col - 2)
    mark("entry2")

    def swap_state(n):
        remote(state.at[n], pair.at[n], send_sem.at[0], pair_sem.at[n], {"row": partner})

    swap_state(0)
    for i, (src, dst) in enumerate(norms):
        remote(dst.at[0], dst.at[1], send_sem.at[6], pw_sem.at[0, 3 + n_chip + i], {"row": partner})
    share_qkv(0)
    load_cache(0)
    loads["rest", 0] = load_rest(0)

    def own_head(vec_ref, l):
        total = jnp.zeros((1, head), F32)
        for j in range(n_row):
            total = total + jnp.where(me == j, vec_ref[l:l + 1, j * head:(j + 1) * head].astype(F32), 0.0)
        return total

    def side_operand(gain, shift, l):
        both = [jnp.concatenate([ref[0, l:l + 1], ref[1, l:l + 1]], axis=1).astype(F32) for ref in (gain, shift)]
        sub = lax.broadcasted_iota(jnp.int32, (16, near), 0)
        return jnp.where(sub == 0, both[0], jnp.where(sub == 1, both[1], 0.0)).astype(BF16)

    low = lax.broadcasted_iota(jnp.int32, (rows, lanes), 1) < head
    low_half = low[0:half]
    low8 = low[0:8]

    def split(q, k):
        q_own = jnp.where(core == 0, q, pltpu.roll(q, head, axis=1))
        k_own = jnp.where(core == 0, pltpu.roll(k, head, axis=1), k)
        return jnp.where(low[0:q.shape[0]], q_own, k_own)

    def qkv_tile(lhs, l, i):
        at = pl.ds(pl.multiple_of(dests[i] * lanes, lanes), lanes)
        return [jnp.dot(lhs, w[l, :, at], preferred_element_type=F32) for w in (wq, wk, wv)]

    def qkv_side(l):
        lhs = side_operand(ln1g, ln1b, l)
        for i in range(n_chip):
            q, k, v = qkv_tile(lhs, l, i)
            both = split(q, k)[0:8]
            vs = split(v, v)[0:8]
            vs = pltpu.roll(vs, 2, axis=0)
            sub = lax.broadcasted_iota(jnp.int32, (8, lanes), 0)
            cq_src[l, i] = jnp.where(sub < 2, both, vs)
            if i < far:
                remote(cq_src.at[l, i], cq_in.at[l, i], send_sem.at[1], cq_sem.at[l, i], {"row": dests[i] * 2 + core})

    def up_side(l):
        lhs = side_operand(ln2g, ln2b, l)
        for i in range(n_chip):
            cu_src[l, i] = jnp.dot(lhs, w1[l, i], preferred_element_type=F32)[0:8]
            if i < far:
                remote(cu_src.at[l, i], cu_in.at[l, i], send_sem.at[1], cu_sem.at[l, i], {"row": dests[i] * 2 + core})

    def normalize(n, gain, shift, l):
        await_recv(pair.at[n], pair_sem.at[n])
        mark("norm")
        xs = [state[n].astype(F32), pair[n].astype(F32)]
        s1 = jnp.sum(xs[0], axis=1, keepdims=True) + jnp.sum(xs[1], axis=1, keepdims=True)
        s2 = jnp.sum(xs[0] * xs[0], axis=1, keepdims=True) + jnp.sum(xs[1] * xs[1], axis=1, keepdims=True)
        mean = s1 / near
        inv = lax.rsqrt(jnp.maximum(s2 / near - mean * mean, 0.0) + EPS_LN)
        z = jnp.concatenate([((x - mean) * inv * gain[i, l:l + 1].astype(F32)).astype(BF16)
                             for i, x in enumerate(xs)], axis=1)
        return z, s1, s2

    def send_stats(n, s1, s2):
        lane = lax.broadcasted_iota(jnp.int32, (rows, 128), 1)
        both = jnp.where(lane == 0, s1, jnp.where(lane == 1, s2, 0.0))
        stat_src[n] = jnp.transpose(both)[0:8]
        for i in range(far):
            remote(stat_src.at[n], stat_in.at[n, i], send_sem.at[1], stat_sem.at[n, i], {"row": dests[i] * 2 + core})

    def stat_columns(n):
        for i in range(far):
            await_recv(stat_in.at[n, i], stat_sem.at[n, i])
        parts = [stat_in[n, i] for i in range(far)] + [stat_src[n]]
        total = parts[0]
        for part in parts[1:]:
            total = total + part
        mean = total[0:1] / width
        inv = lax.rsqrt(total[1:2] / width - mean * mean + EPS_LN)
        scales, shifts = [], []
        for part in parts:
            near_mean = part[0:1] / near
            near_var = jnp.maximum(part[1:2] / near - near_mean * near_mean, 0.0) + EPS_LN
            scales.append(inv * (near_var * lax.rsqrt(near_var)))
            shifts.append(inv * (near_mean - mean))
        table = jnp.concatenate(scales + shifts + [jnp.zeros((128 - 2 * n_chip, rows), F32)], axis=0)
        columns = jnp.transpose(table)
        return ([columns[:, i:i + 1] for i in range(n_chip)],
                [columns[:, n_chip + i:n_chip + i + 1] for i in range(n_chip)])

    len_col = jnp.transpose(jnp.broadcast_to(len_buf[...], (rows, rows)))[:, 0:1]

    def all_peers():
        for i in range(far):
            for e in range(2):
                yield dests[i] * 2 + lax.rem(core + e, 2)
        yield partner

    mark("side0")
    for copy in loads["qkv", 0]:
        copy.wait()
    for i in range(4):
        await_recv(norms[i][1].at[1], pw_sem.at[0, 3 + n_chip + i])
    for i, w in enumerate((wq, wk, wv)):
        await_recv(w.at[0, cols:], pw_sem.at[0, i])
    qkv_side(0)

    for l in range(layers):
        n = 2 * l
        if l > 0:
            for copy in loads["qkv", l]:
                copy.wait()
        mark("pair_wait")
        z, s1, s2 = normalize(n, ln1g, ln1b, l)
        mark("qkv_mm")
        for i in range(n_chip):
            q, k, v = qkv_tile(z, l, i)
            v_r = pltpu.roll(v, head, axis=1)
            low_v = jnp.where(core == 0, v, v_r)
            high_v = jnp.where(core == 0, v_r, v)
            block = qkv_src.at[l, i]
            block[0:rows] = split(q, k).astype(BF16)
            block[rows:] = jnp.where(low_half, low_v[0:half], high_v[half:]).astype(BF16)
            if i < far:
                remote(block, qkv_in.at[l, i], send_sem.at[2], qkv_sem.at[l, i], {"row": dests[i] * 2 + core})
            if i == 0:
                send_stats(n, s1, s2)
        if l == 0:
            share_up(0)
        mark("qkv_wait")
        for i in range(far):
            await_recv(cq_in.at[l, i], cq_sem.at[l, i])
        scales, shifts = stat_columns(n)
        total = jnp.zeros((rows + half, lanes), F32)
        const = jnp.zeros((8, lanes), F32)
        for i in [far] + list(range(far)):
            if i < far:
                await_recv(qkv_in.at[l, i], qkv_sem.at[l, i])
            part = (qkv_in[l, i] if i < far else qkv_src[l, i]).astype(F32)
            side = cq_in[l, i] if i < far else cq_src[l, i]
            scale_v = jnp.where(low_half, scales[i][0:half], scales[i][half:])
            shift_v = jnp.where(low_half, shifts[i][0:half], shifts[i][half:])
            total = total + jnp.concatenate([part[0:rows] * scales[i] + shifts[i] * side[0:1],
                                             part[rows:] * scale_v + shift_v * side[2:3]], axis=0)
            const = const + side
        mark("qkv_sum")
        qk = total[0:rows] + const[1:2]
        vv = total[rows:] + const[3:4]
        q_b = ((qk[:, 0:head] + own_head(bq, l)) * (head ** -0.5)).astype(BF16)
        k_new = (pltpu.roll(qk, head, axis=1)[:, 0:head] + own_head(bk, l)).astype(BF16)
        v_new = (jnp.concatenate([vv[:, 0:head], pltpu.roll(vv, head, axis=1)[:, 0:head]], axis=0)
                 + own_head(bv, l)).astype(BF16)
        q_f = q_b.astype(F32)
        k_f = k_new.astype(F32)
        twin[...] = jnp.concatenate([q_f, q_f], axis=1).astype(BF16)
        k_out[l] = jnp.transpose(k_f).astype(BF16)
        v_t = jnp.transpose(v_new.astype(F32))
        v_out[l] = v_t.astype(BF16)
        score_new = jnp.sum(q_f * k_f, axis=1, keepdims=True)

        mark("scores")

        def score_step(t, carry, l=l):
            for u in range(2):
                cache_copy(l, 0, 2 * t + u).wait()
            for u in range(2):
                at = pl.ds(pl.multiple_of(32 * t + 16 * u, 16), 16)
                q_diag = jnp.concatenate([twin[at, :]] * (16 * head // lanes), axis=1) * onehot[...]
                keys = k_buf[l, pl.ds(32 * t + 16 * u, 16)].reshape(16 * head, s_max)
                scores[at, :] = jnp.dot(q_diag, keys, preferred_element_type=F32)
            return carry

        lax.fori_loop(0, steps // 2, score_step, 0)
        mark("softmax")
        sc = scores[...]
        position = lax.broadcasted_iota(jnp.int32, sc.shape, 1)
        sc = jnp.where(position < len_col, sc, -jnp.inf)
        peak = jnp.maximum(jnp.max(sc, axis=1, keepdims=True), score_new)
        ex = jnp.exp(sc - peak)
        ex_new = jnp.exp(score_new - peak)
        mass = jnp.sum(ex, axis=1, keepdims=True) + ex_new
        scores[...] = ex / mass
        prob_new = (ex_new / mass).astype(BF16).astype(F32)
        for b in range(s_max // 128):
            probs_t[b * 128:(b + 1) * 128, :] = jnp.transpose(scores[:, b * 128:(b + 1) * 128]).astype(BF16)
        prob_row = jnp.transpose(jnp.broadcast_to(prob_new, (rows, 128)))[0:1, :]
        lane64 = lax.broadcasted_iota(jnp.int32, (head, rows), 1)
        mark("mix")

        def mix_step(t, acc, l=l):
            for u in range(2):
                cache_copy(l, 1, 2 * t + u).wait()
            values = v_buf[l, pl.ds(32 * t, 32)].reshape(32 * head, s_max)
            full = jnp.dot(values, probs_t[...], preferred_element_type=F32)
            for i in range(32):
                acc = jnp.where(lane64 == 32 * t + i, full[i * head:(i + 1) * head], acc)
            return acc

        mixed = lax.fori_loop(0, steps // 2, mix_step, jnp.zeros((head, rows), F32))
        mark("att_send")
        att_in[l, me] = (mixed + prob_row * v_t).astype(BF16)
        for target in all_peers():
            remote(att_in.at[l, me], att_in.at[l, me], send_sem.at[3], att_sem.at[l, me], {"row": target})
        mark("att_wait")
        if l + 1 < layers:
            loads["qkv", l + 1] = load_qkv(l + 1)
            load_cache(l + 1)
            loads["rest", l + 1] = load_rest(l + 1)
            share_qkv(l + 1)
            share_up(l + 1)
        for copy in loads["rest", l]:
            copy.wait()
        for i in range(n_chip):
            await_recv(w1.at[l, i, cols:], pw_sem.at[l, 3 + i])
        up_side(l)
        for k in range(1, n_row):
            j = lax.rem(me + k, n_row)
            await_recv(att_in.at[l, j], att_sem.at[l, j])
        mark("wo_mm")
        gathered = att_in[l].reshape(n_row * head, rows)
        part = lax.dot_general(gathered, wo[l], (((0,), (0,)), ((), ())), preferred_element_type=F32)
        proj_in[l, mine] = part.astype(BF16)

        def all_reduce_col(buf, sem, bias, base):
            mark("col_send")
            for k in (2, 1, 3) if n_col == 4 else range(1, n_col):
                remote(buf.at[l, mine], buf.at[l, mine], send_sem.at[4], sem.at[l, mine],
                       {"col": lax.rem(mine + k, n_col)})
            mark("col_wait")
            for k in range(1, n_col):
                j = lax.rem(mine + k, n_col)
                await_recv(buf.at[l, j], sem.at[l, j])
            mark("col_sum")
            summed = buf[l, 0].astype(F32)
            for j in range(1, n_col):
                summed = summed + buf[l, j].astype(F32)
            return (base.astype(F32) + (summed + bias.astype(F32))).astype(BF16)

        state[n + 1] = all_reduce_col(proj_in, proj_sem, bo[l:l + 1, :], state[n])
        swap_state(n + 1)
        mark("pair_wait")
        z, s1, s2 = normalize(n + 1, ln2g, ln2b, l)
        mark("up_mm")
        for i in range(n_chip):
            up_src[l, i] = jnp.dot(z, w1[l, i], preferred_element_type=F32).astype(BF16)
            if i < far:
                remote(up_src.at[l, i], up_in.at[l, i], send_sem.at[2], up_sem.at[l, i], {"row": dests[i] * 2 + core})
            if i == 0:
                send_stats(n + 1, s1, s2)
        mark("up_wait")
        if l + 1 < layers:
            for i, w in enumerate((wq, wk, wv)):
                await_recv(w.at[l + 1, cols:], pw_sem.at[l + 1, i])
            for copy in loads["qkv", l + 1]:
                copy.wait()
            loads["qkv", l + 1] = []
            qkv_side(l + 1)
        for i in range(far):
            await_recv(cu_in.at[l, i], cu_sem.at[l, i])
        scales, shifts = stat_columns(n + 1)
        total = jnp.zeros((rows, ff), F32)
        const = jnp.zeros((8, ff), F32)
        for i in [far] + list(range(far)):
            if i < far:
                await_recv(up_in.at[l, i], up_sem.at[l, i])
            part = (up_in[l, i] if i < far else up_src[l, i]).astype(F32)
            side = cu_in[l, i] if i < far else cu_src[l, i]
            total = total + (part * scales[i] + shifts[i] * side[0:1])
            const = const + side
        mark("up_sum")
        own_at = pl.ds(pl.multiple_of(me * ff, ff), ff)
        bias = b1[l:l + 1, own_at].astype(F32)
        act_in[l, me] = jnp.maximum((total + const[1:2] + bias).astype(BF16), 0)
        for i in range(far):
            remote(act_in.at[l, me], act_in.at[l, me], send_sem.at[5], act_sem.at[l, me], {"row": dests[i] * 2 + core})
        remote(act_in.at[l, me], act_in.at[l, me], send_sem.at[5], act_sem.at[l, me], {"row": partner})
        mark("act_wait")

        def down(j):
            return jnp.dot(act_in[l, j], w2[l, pl.ds(pl.multiple_of(j * ff, ff), ff), :], preferred_element_type=F32)

        part = down(me)
        await_recv(act_in.at[l, partner], act_sem.at[l, partner])
        part = part + down(partner)
        arrivals = [lax.rem(chip + n_chip - dc, n_chip) * 2 for dc in sorted(hops, key=lambda d: min(d, n_chip - d))]
        for j in arrivals:
            j = j + core
            await_recv(act_in.at[l, j], act_sem.at[l, j])
            remote(act_in.at[l, j], act_in.at[l, j], send_sem.at[5], act_sem.at[l, j], {"row": partner})
            part = part + down(j)
        for j in arrivals:
            j = j + 1 - core
            await_recv(act_in.at[l, j], act_sem.at[l, j])
            part = part + down(j)
        mark("down_mm")
        down_in[l, mine] = part.astype(BF16)
        new_state = all_reduce_col(down_in, down_sem, b2[l:l + 1, :], state[n + 1])
        if l + 1 < layers:
            state[n + 2] = new_state
            swap_state(n + 2)
        else:
            h_out[...] = new_state
    mark("tail")
    for copy in pending:
        copy.wait_send()
    mark(None)


def store(*refs):
    copies = [pltpu.make_async_copy(refs[i], refs[3 + i], refs[6].at[i]) for i in range(3)]
    for copy in copies:
        copy.start()
    for copy in copies:
        copy.wait()


def solution(mesh):
    n_row = mesh.shape["row"]
    n_col = mesh.shape["col"]
    act_spec = P("dp", "row")
    cache_spec = P(None, "dp", ("col", "row"), None, None)
    fresh_spec = P(None, "dp", ("col", "row"), None)
    in_weight = P(None, "row", "col")
    out_weight = P(None, "col", "row")
    col_vec = P(None, "col")
    row_vec = P(None, "row")
    in_specs = (act_spec, P("dp"), cache_spec, cache_spec, row_vec, row_vec,
                in_weight, col_vec, in_weight, col_vec, in_weight, col_vec,
                out_weight, row_vec, row_vec, row_vec, in_weight, col_vec, out_weight, row_vec)

    def local_step(hidden, cache_len, k_cache, v_cache, *params):
        rows, cols = hidden.shape
        layers, _, _, s_max, head = k_cache.shape
        keys = jnp.swapaxes(k_cache, 3, 4).reshape(layers, rows, head, s_max)
        values = jnp.swapaxes(v_cache, 3, 4).reshape(layers, rows, head, s_max)
        operands = (hidden, cache_len.reshape(1, rows), keys, values) + params
        dma = pltpu.SemaphoreType.DMA
        ff = params[12].shape[2]
        cols2 = 2 * cols
        n_chip = n_row // 2
        ff_own = ff // n_row
        shapes = [a.shape for a in operands]
        shapes = shapes[1:4] + [(2,) + s if i in (0, 1, 10, 11) else s for i, s in enumerate(shapes[4:])]
        for i in (5, 7, 9):
            shapes[i] = (layers, cols2, shapes[i][2])
        shapes[15] = (layers, n_chip, cols2, ff_own)
        vmem = [pltpu.VMEM(s, a.dtype) for s, a in zip(shapes, operands[1:])]
        scratch = vmem + [
            pltpu.VMEM((2 * layers, rows, cols), BF16),
            pltpu.VMEM((2 * layers, rows, cols), BF16),
            pltpu.VMEM((2 * layers, 8, rows), F32),
            pltpu.VMEM((2 * layers, n_chip - 1, 8, rows), F32),
            pltpu.VMEM((layers, n_chip, 8, 2 * head), F32),
            pltpu.VMEM((layers, n_chip - 1, 8, 2 * head), F32),
            pltpu.VMEM((layers, n_chip, 8, ff_own), F32),
            pltpu.VMEM((layers, n_chip - 1, 8, ff_own), F32),
            pltpu.VMEM((layers, n_chip, rows + rows // 2, 2 * head), BF16),
            pltpu.VMEM((layers, n_chip - 1, rows + rows // 2, 2 * head), BF16),
            pltpu.VMEM((layers, n_row, head, rows), BF16),
            pltpu.VMEM((layers, n_col, rows, cols), BF16),
            pltpu.VMEM((layers, n_chip, rows, ff_own), BF16),
            pltpu.VMEM((layers, n_chip - 1, rows, ff_own), BF16),
            pltpu.VMEM((layers, n_row, rows, ff_own), BF16),
            pltpu.VMEM((layers, n_col, rows, cols), BF16),
            pltpu.VMEM((rows, 2 * head), BF16),
            pltpu.VMEM((16, 16 * head), BF16),
            pltpu.VMEM((rows, s_max), F32),
            pltpu.VMEM((s_max, rows), BF16),
            dma((1 + layers, 12)),
            dma((layers, 2, rows // 16)),
            dma((8,)),
            dma((layers, 7 + n_chip)),
            dma((2 * layers,)),
            dma((2 * layers, n_chip - 1)),
            dma((layers, n_chip - 1)),
            dma((layers, n_chip - 1)),
            dma((layers, n_chip - 1)),
            dma((layers, n_row)),
            dma((layers, n_col)),
            dma((layers, n_chip - 1)),
            dma((layers, n_row)),
            dma((layers, n_col)),
        ]
        h, kt, vt = pl.pallas_call(
            functools.partial(kernel, n_row, n_col, cols * n_row),
            out_shape=(pltpu.VMEM((rows, cols), BF16),
                       pltpu.VMEM((layers, head, rows), BF16),
                       pltpu.VMEM((layers, head, rows), BF16)),
            in_specs=[pl.BlockSpec(memory_space=pltpu.HBM)] * len(operands),
            out_specs=[pl.BlockSpec(memory_space=pltpu.VMEM)] * 3,
            scratch_shapes=scratch,
            compiler_params=pltpu.CompilerParams(collective_id=0, has_side_effects=True,
                                                 vmem_limit_bytes=63 * 2 ** 20),
        )(*operands)
        h, kt, vt = pl.pallas_call(
            store,
            out_shape=(jax.ShapeDtypeStruct((rows, cols), BF16),
                       jax.ShapeDtypeStruct((layers, head, rows), BF16),
                       jax.ShapeDtypeStruct((layers, head, rows), BF16)),
            in_specs=[pl.BlockSpec(memory_space=pltpu.VMEM)] * 3,
            out_specs=[pl.BlockSpec(memory_space=pltpu.HBM)] * 3,
            scratch_shapes=[dma((3,))],
        )(*[pltpu.with_memory_space_constraint(a, pltpu.VMEM) for a in (h, kt, vt)])
        k_new = jnp.swapaxes(kt, 1, 2).reshape(layers, rows, 1, head)
        v_new = jnp.swapaxes(vt, 1, 2).reshape(layers, rows, 1, head)
        return h, k_new, v_new

    return jax.shard_map(local_step, mesh=mesh, in_specs=in_specs,
                         out_specs=(act_spec, fresh_spec, fresh_spec), check_vma=False)
```

time: 557 us -> 91.6 us (0.16)
  waiting for transfers between devices: 388 us -> 0 us
  blocking collectives: 94.9 us -> 0 us
  Pallas kernels: 0 us -> 90.9 us
  matrix products: 40.1 us -> 0 us
  other arithmetic: 14.4 us -> 0 us
  between operations: 14.5 us -> 0.65 us
    psum x6 -> x0, waiting for transfers between devices: 255 us -> none  [the longest x2 103 us: local_step(): inner_sum = lax.psum(inner_part, 'row')]
    reduce_scatter x6 -> x0, waiting for transfers between devices: 132 us -> none  [head_projection(): summed = lax.psum_scatter(partial, 'row', scatter_dimension=1, tiled=True)]
    pallas_call x0 -> x2, Pallas kernels: none -> 90.9 us  [the longest x1 90.2 us: local_step(): pl.pallas_call(functools.partial(kernel, n_row, n_col, cols * n_row), out...]
    psum x4 -> x0, blocking collectives: 57.3 us -> none  [layer_norm(): stats = lax.psum(stats, 'row')]
    dot_general x16 -> x0, matrix products: 40.1 us -> none  [the longest x2 11.3 us: attention(): jnp.einsum('bhs,bhsd->bhd', prob_cache, v_layer, preferred_element_type=j...]
    all_gather x2 -> x0, blocking collectives: 37.6 us -> none  [local_step(): lax.all_gather(attended.reshape(batch_rows, heads_dev * head_dim), 'row',...]
  transfers between devices with their start and end apart: 12 -> 0, of which waited for: 12 -> 0; matrix products, arithmetic and copies ran while one was open for 7% -> 0% of each run, Pallas kernels for 0% -> 0%
where the time goes in v2:
time: 91.6 us; the launch traced here: 91.5 us
  Pallas kernels  90.9 us (99%)
    pallas_call x1, Pallas kernels, local_step(): pl.pallas_call(functools.partial(kernel, n_row, n_col, cols * n_row), out...  90.2 us

profile of v2, /device:TPU:97, one launch (start us, length us, event | category | flops | bytes accessed | tf_op | source)
XLA Modules:
  0.0 91.5 jit_solution(7827854185933265998)
XLA Ops:
  0.6 90.2 %shard_map.211 = (bf16[128,256]{1,0:T(8,128)(2,1)S(1)}, bf16[2,64,128]{2,1,0:T(8,128)(2,1)S(1)}, bf16[2,64,128]{2,1,0:T(8,128)(2,1)S(1)}) custom-call(bf16[128,256]{1,0:T(8,128)(2,1)} %x_hbm.1, s32[1,128]{1,0:T(1,128)} %bitcast.23, bf16[2,128,64,512]{3,2,1,0:T(8,128)(2,1)} %bitcast.21, bf16[2,128,64,512]{3,2,1,0:T(8,128)(2,1)} %bitcast.22, ...), custom_call_target="tpu_custom_call" | custom-call | tf_op jit(solution)/shard_map/pallas_call | solution.py:512
  90.9 0.7 shard_map.212

commit v3 on v2

v3 whole, which is shorter than its diff:
```python
import functools

import jax
import jax.numpy as jnp
from jax import lax
from jax.experimental import pallas as pl
from jax.experimental.pallas import tpu as pltpu
from jax.sharding import PartitionSpec as P

EPS_LN = 1e-5
F32 = jnp.float32
BF16 = jnp.bfloat16
MESH = pl.DeviceIdType.MESH


class Marks:
    def __init__(self):
        self.open = None

    def __call__(self, name):
        if self.open is not None:
            self.open.__exit__(None, None, None)
        self.open = None
        if name:
            self.open = jax.named_scope(name)
            self.open.__enter__()


HALVES = 2


def kernel(n_row, n_col, width,
           x_hbm, len_hbm, k_hbm, v_hbm, ln1g_hbm, ln1b_hbm, wq_hbm, bq_hbm, wk_hbm, bk_hbm, wv_hbm, bv_hbm,
           wo_hbm, bo_hbm, ln2g_hbm, ln2b_hbm, w1_hbm, b1_hbm, w2_hbm, b2_hbm,
           h_out, k_out, v_out,
           len_buf, k_buf, v_buf, ln1g, ln1b, wq, bq, wk, bk, wv, bv, wo, bo, ln2g, ln2b, w1, b1, w2, b2,
           state, pair, stat_src, stat_in, cq_src, cq_in, cu_src, cu_in, w_in, w_share,
           qkv_src, qkv_in, att_in, proj_in, up_src, up_in, act_in, down_in,
           twin, onehot, scores, probs_t,
           in_sem, kv_sem, send_sem, pw_sem, pair_sem, stat_sem, cq_sem, cu_sem,
           qkv_sem, att_sem, proj_sem, up_sem, act_sem, down_sem):
    mark = Marks()
    mark("entry")
    layers = wo.shape[0]
    rows, cols = state.shape[2:]
    batch = rows * HALVES
    head = k_buf.shape[2]
    s_max = k_buf.shape[3]
    lanes = 2 * head
    half = rows // 2
    n_chip = n_row // 2
    near = width // n_chip
    ff = w1.shape[3]
    me = lax.axis_index("row")
    mine = lax.axis_index("col")
    chip = me // 2
    core = lax.rem(me, 2)
    partner = chip * 2 + (1 - core)
    hops = [2, 1, 3]
    far = len(hops)
    dests = [lax.rem(chip + dc, n_chip) for dc in hops] + [chip]
    peers = [dest * 2 + core for dest in dests[:far]]
    arrivals = [lax.rem(chip + n_chip - dc, n_chip) * 2 for dc in (1, 3, 2)]
    pending = []

    def local(src, dst, sem):
        copy = pltpu.make_async_copy(src, dst, sem)
        copy.start()
        return copy

    def remote(src, dst, ssem, rsem, target):
        copy = pltpu.make_async_remote_copy(src_ref=src, dst_ref=dst, send_sem=ssem, recv_sem=rsem,
                                            device_id=target, device_id_type=MESH)
        copy.start()
        pending.append(copy)

    def await_recv(dst, sem):
        pltpu.make_async_remote_copy(src_ref=dst, dst_ref=dst, send_sem=sem, recv_sem=sem,
                                     device_id={"row": me}, device_id_type=MESH).wait_recv()

    def cache_copy(l, which, t):
        src, dst = ((k_hbm, k_buf), (v_hbm, v_buf))[which]
        return pltpu.make_async_copy(src.at[l, pl.ds(16 * t, 16)], dst.at[l, pl.ds(16 * t, 16)], kv_sem.at[l, which, t])

    norms = [(ln1g_hbm, ln1g), (ln1b_hbm, ln1b), (ln2g_hbm, ln2g), (ln2b_hbm, ln2b)]
    smalls = ([(len_hbm, len_buf), (bq_hbm, bq), (bk_hbm, bk), (bv_hbm, bv), (bo_hbm, bo), (b1_hbm, b1), (b2_hbm, b2)]
              + [(src, dst.at[0]) for src, dst in norms]
              + [(x_hbm.at[h * rows:(h + 1) * rows], state.at[0, h]) for h in range(HALVES)])
    small_copies = [local(src, dst, in_sem.at[0, i]) for i, (src, dst) in enumerate(smalls)]

    def load_qkv(l):
        return [local(src.at[l], dst.at[l], in_sem.at[1 + l, i])
                for i, (src, dst) in enumerate([(wq_hbm, wq), (wk_hbm, wk), (wv_hbm, wv)])]

    loads = {("qkv", 0): load_qkv(0)}
    barrier = pltpu.get_barrier_semaphore()
    for k in range(1, n_row):
        pl.semaphore_signal(barrier, inc=1, device_id={"row": lax.rem(me + k, n_row)}, device_id_type=MESH)
    for k in range(1, n_col):
        pl.semaphore_signal(barrier, inc=1, device_id={"col": lax.rem(mine + k, n_col)}, device_id_type=MESH)

    def up_columns(i, which):
        return pl.ds(pl.multiple_of((dests[i] * 2 + which) * ff, ff), ff)

    def load_rest(l):
        got = [local(wo_hbm.at[l, :, i], wo.at[l, i], in_sem.at[1 + l, 3 + i]) for i in range(2)]
        got.append(local(w2_hbm.at[l], w2.at[l], in_sem.at[1 + l, 5]))
        return got + [local(w1_hbm.at[l, :, up_columns(i, core)], w1.at[l, i, 0:cols], in_sem.at[1 + l, 6 + i])
                      for i in range(n_chip)]

    def share_up(l):
        for i in range(n_chip):
            remote(w1_hbm.at[l, :, up_columns(i, 1 - core)], w1.at[l, i, cols:], send_sem.at[7], pw_sem.at[l, 1 + i],
                   {"row": partner})

    def load_cache(l):
        for which in range(2):
            for t in range(batch // 16):
                cache_copy(l, which, t).start()

    low = lax.broadcasted_iota(jnp.int32, (cols, lanes), 1) < head
    low_half = low[0:half]

    def repack(l):
        def tile(w, i):
            return w[l, :, pl.ds(pl.multiple_of(dests[i] * lanes, lanes), lanes)].astype(F32)

        pairs = [(wq, 0, wk, 0), (wv, 0, wv, 1), (wq, 1, wk, 1), (wq, 2, wk, 2), (wv, 2, wv, 3), (wq, 3, wk, 3)]
        for t, (wa, ia, wb, ib) in enumerate(pairs):
            a, b = tile(wa, ia), tile(wb, ib)
            first = jnp.where(low, a, pltpu.roll(b, head, axis=1)).astype(BF16)
            second = jnp.where(low, pltpu.roll(a, head, axis=1), b).astype(BF16)
            at = slice(t * lanes, (t + 1) * lanes)
            w_in[l, 0:cols, at] = jnp.where(core == 0, first, second)
            w_share[l, :, at] = jnp.where(core == 0, second, first)

    def share_qkv(l):
        remote(w_share.at[l], w_in.at[l, cols:], send_sem.at[6], pw_sem.at[l, 0], {"row": partner})

    def swap_state(n, h):
        remote(state.at[n, h], pair.at[n, h], send_sem.at[0], pair_sem.at[n, h], {"row": partner})

    lane_id = lax.broadcasted_iota(jnp.int32, (16, 16 * head), 1)
    row_id = lax.broadcasted_iota(jnp.int32, (16, 16 * head), 0)
    onehot[...] = jnp.where(lane_id // head == row_id, 1.0, 0.0).astype(BF16)
    for copy in small_copies:
        copy.wait()
    mark("load0")
    for copy in loads["qkv", 0]:
        copy.wait()
    load_cache(0)
    loads["rest", 0] = load_rest(0)
    mark("repack0")
    repack(0)
    mark("barrier")
    pl.semaphore_wait(barrier, n_row + n_col - 2)
    mark("entry2")
    for h in range(HALVES):
        swap_state(0, h)
    for i, (src, dst) in enumerate(norms):
        remote(dst.at[0], dst.at[1], send_sem.at[6], pw_sem.at[0, 1 + n_chip + i], {"row": partner})
    share_qkv(0)

    def own_head(vec_ref, l):
        total = jnp.zeros((1, head), F32)
        for j in range(n_row):
            total = total + jnp.where(me == j, vec_ref[l:l + 1, j * head:(j + 1) * head].astype(F32), 0.0)
        return total

    def side_operand(gain, shift, l):
        both = [jnp.concatenate([ref[0, l:l + 1], ref[1, l:l + 1]], axis=1).astype(F32) for ref in (gain, shift)]
        sub = lax.broadcasted_iota(jnp.int32, (16, near), 0)
        return jnp.where(sub == 0, both[0], jnp.where(sub == 1, both[1], 0.0)).astype(BF16)

    def qkv_products(lhs, l):
        wide = 2 * lanes
        for t in range(3):
            full = jnp.dot(lhs, w_in[l, :, t * wide:(t + 1) * wide], preferred_element_type=F32)
            yield full[:, 0:lanes], full[:, lanes:]

    def qkv_blocks(lhs, l):
        tiles = qkv_products(lhs, l)
        qk0, v01 = next(tiles)
        yield qk0, v01, 0
        qk1, qk2 = next(tiles)
        yield qk1, v01, 1
        v23, qk3 = next(tiles)
        yield qk2, v23, 0
        yield qk3, v23, 1

    def qkv_side(l):
        lhs = side_operand(ln1g, ln1b, l)
        for i, (qk, v, side) in enumerate(qkv_blocks(lhs, l)):
            v, low8 = v[0:8], low[0:8]
            v_r = pltpu.roll(v, head, axis=1)
            vs = jnp.where(low8, v, v_r) if side == 0 else jnp.where(low8, v_r, v)
            sub = lax.broadcasted_iota(jnp.int32, (8, lanes), 0)
            cq_src[l, i] = jnp.where(sub < 2, qk[0:8], pltpu.roll(vs, 2, axis=0))
            if i < far:
                remote(cq_src.at[l, i], cq_in.at[l, i], send_sem.at[1], cq_sem.at[l, i], {"row": peers[i]})

    def up_side(l):
        lhs = side_operand(ln2g, ln2b, l)
        for i in range(n_chip):
            cu_src[l, i] = jnp.dot(lhs, w1[l, i], preferred_element_type=F32)[0:8]
            if i < far:
                remote(cu_src.at[l, i], cu_in.at[l, i], send_sem.at[1], cu_sem.at[l, i], {"row": peers[i]})

    def normalize(n, h, gain, l):
        await_recv(pair.at[n, h], pair_sem.at[n, h])
        mark("norm")
        xs = [state[n, h].astype(F32), pair[n, h].astype(F32)]
        s1 = jnp.sum(xs[0] + xs[1], axis=1, keepdims=True)
        s2 = jnp.sum(xs[0] * xs[0] + xs[1] * xs[1], axis=1, keepdims=True)
        mean = s1 / near
        inv = lax.rsqrt(jnp.maximum(s2 / near - mean * mean, 0.0) + EPS_LN)
        z = jnp.concatenate([((x - mean) * inv * gain[i, l:l + 1].astype(F32)).astype(BF16)
                             for i, x in enumerate(xs)], axis=1)
        return z, s1, s2

    def send_stats(n, h, s1, s2):
        lane = lax.broadcasted_iota(jnp.int32, (rows, 128), 1)
        both = jnp.where(lane == 0, s1, jnp.where(lane == 1, s2, 0.0))
        both = jnp.concatenate([both, jnp.zeros((128 - rows, 128), F32)], axis=0)
        stat_src[n, h] = jnp.transpose(both)[0:8]
        for i in range(far):
            remote(stat_src.at[n, h], stat_in.at[n, h, i], send_sem.at[1], stat_sem.at[n, h, i], {"row": peers[i]})

    def stat_columns(n, h):
        for i in range(far):
            await_recv(stat_in.at[n, h, i], stat_sem.at[n, h, i])
        parts = [stat_in[n, h, i] for i in range(far)] + [stat_src[n, h]]
        total = parts[0]
        for part in parts[1:]:
            total = total + part
        mean = total[0:1] / width
        inv = lax.rsqrt(total[1:2] / width - mean * mean + EPS_LN)
        scales, shifts = [], []
        for part in parts:
            near_mean = part[0:1] / near
            near_var = jnp.maximum(part[1:2] / near - near_mean * near_mean, 0.0) + EPS_LN
            scales.append(inv * (near_var * lax.rsqrt(near_var)))
            shifts.append(inv * (near_mean - mean))
        table = jnp.concatenate(scales + shifts + [jnp.zeros((128 - 2 * n_chip, 128), F32)], axis=0)
        columns = jnp.transpose(table)[0:rows]
        return ([columns[:, i:i + 1] for i in range(n_chip)],
                [columns[:, n_chip + i:n_chip + i + 1] for i in range(n_chip)])

    len_all = jnp.transpose(jnp.broadcast_to(len_buf[...], (batch, batch)))
    fresh = {}

    def qkv_go(l, h):
        n = 2 * l
        mark("pair_wait")
        z, s1, s2 = normalize(n, h, ln1g, l)
        mark("qkv_mm")
        for i, (qk, v, side) in enumerate(qkv_blocks(z, l)):
            v_r = pltpu.roll(v, head, axis=1)
            a, b = (v, v_r) if side == 0 else (v_r, v)
            block = qkv_src.at[l, h, i]
            block[0:rows] = qk.astype(BF16)
            block[rows:] = jnp.where(low_half, a[0:half], b[half:]).astype(BF16)
            if i < far:
                remote(block, qkv_in.at[l, h, i], send_sem.at[2], qkv_sem.at[l, h, i], {"row": peers[i]})
            if i == 0:
                send_stats(n, h, s1, s2)

    def qkv_recv(l, h):
        mark("qkv_wait")
        for i in range(far if h == 0 else 0):
            await_recv(cq_in.at[l, i], cq_sem.at[l, i])
        scales, shifts = stat_columns(2 * l, h)
        qk = jnp.zeros((rows, lanes), F32)
        vv = jnp.zeros((half, lanes), F32)
        const = jnp.zeros((8, lanes), F32)
        for i in (far, 1, 2, 0):
            if i < far:
                await_recv(qkv_in.at[l, h, i], qkv_sem.at[l, h, i])
            block = qkv_in.at[l, h, i] if i < far else qkv_src.at[l, h, i]
            side = cq_in[l, i] if i < far else cq_src[l, i]
            scale_v = jnp.where(low_half, scales[i][0:half], scales[i][half:])
            shift_v = jnp.where(low_half, shifts[i][0:half], shifts[i][half:])
            qk = qk + (block[0:rows].astype(F32) * scales[i] + shifts[i] * side[0:1])
            vv = vv + (block[rows:].astype(F32) * scale_v + shift_v * side[2:3])
            const = const + side
        mark("qkv_sum")
        qk = qk + const[1:2]
        vv = vv + const[3:4]
        q_b = ((qk[:, 0:head] + own_head(bq, l)) * (head ** -0.5)).astype(BF16)
        k_new = (pltpu.roll(qk, head, axis=1)[:, 0:head] + own_head(bk, l)).astype(BF16)
        v_new = (jnp.concatenate([vv[:, 0:head], pltpu.roll(vv, head, axis=1)[:, 0:head]], axis=0)
                 + own_head(bv, l)).astype(BF16)
        q_f = q_b.astype(F32)
        k_f = k_new.astype(F32)
        mine_rows = slice(h * rows, (h + 1) * rows)
        twin[mine_rows, :] = jnp.concatenate([q_f, q_f], axis=1).astype(BF16)
        k_out[l, :, mine_rows] = jnp.transpose(k_f).astype(BF16)
        v_t = jnp.transpose(v_new.astype(F32))
        v_out[l, :, mine_rows] = v_t.astype(BF16)
        fresh[l, h] = (jnp.sum(q_f * k_f, axis=1, keepdims=True), v_t)

    def attend(l, h):
        score_new, v_t = fresh[l, h]
        base = h * rows
        mark("scores")

        def score_step(t, carry):
            for u in range(2):
                cache_copy(l, 0, base // 16 + 2 * t + u).wait()
            for u in range(2):
                at = pl.ds(pl.multiple_of(base + 32 * t + 16 * u, 16), 16)
                q_diag = jnp.concatenate([twin[at, :]] * (16 * head // lanes), axis=1) * onehot[...]
                keys = k_buf[l, pl.ds(base + 32 * t + 16 * u, 16)].reshape(16 * head, s_max)
                scores[at, :] = jnp.dot(q_diag, keys, preferred_element_type=F32)
            return carry

        lax.fori_loop(0, rows // 32, score_step, 0)
        mark("softmax")
        mine_rows = slice(base, base + rows)
        sc = scores[mine_rows, :]
        position = lax.broadcasted_iota(jnp.int32, sc.shape, 1)
        sc = jnp.where(position < len_all[mine_rows, 0:1], sc, -jnp.inf)
        peak = jnp.maximum(jnp.max(sc, axis=1, keepdims=True), score_new)
        ex = jnp.exp(sc - peak)
        ex_new = jnp.exp(score_new - peak)
        mass = jnp.sum(ex, axis=1, keepdims=True) + ex_new
        scores[mine_rows, :] = ex / mass
        prob_new = (ex_new / mass).astype(BF16).astype(F32)
        for b in range(s_max // 128):
            probs_t[h, b * 128:(b + 1) * 128, :] = jnp.transpose(scores[mine_rows, b * 128:(b + 1) * 128]).astype(BF16)
        prob_row = jnp.transpose(jnp.broadcast_to(prob_new, (rows, 128)))[0:1, :]
        lane = lax.broadcasted_iota(jnp.int32, (head, rows), 1)
        mark("mix")

        def mix_step(t, acc):
            for u in range(2):
                cache_copy(l, 1, base // 16 + 2 * t + u).wait()
            values = v_buf[l, pl.ds(base + 32 * t, 32)].reshape(32 * head, s_max)
            full = jnp.dot(values, probs_t[h], preferred_element_type=F32)
            for i in range(32):
                acc = jnp.where(lane == 32 * t + i, full[i * head:(i + 1) * head], acc)
            return acc

        mixed = lax.fori_loop(0, rows // 32, mix_step, jnp.zeros((head, rows), F32))
        mark("att_send")
        mixed = mixed + prob_row * v_t
        att_in[l, h, me] = jnp.concatenate([mixed[0:head // 2], mixed[head // 2:]], axis=1).astype(BF16)
        for target in [d * 2 + lax.rem(core + e, 2) for d in dests[:far] for e in range(2)] + [partner]:
            remote(att_in.at[l, h, me], att_in.at[l, h, me], send_sem.at[3], att_sem.at[l, h, me], {"row": target})

    def col_send(buf, sem, l, h):
        mark("col_send")
        for k in (2, 1, 3):
            remote(buf.at[l, h, mine], buf.at[l, h, mine], send_sem.at[4], sem.at[l, h, mine],
                   {"col": lax.rem(mine + k, n_col)})

    def col_recv(buf, sem, l, h, bias, base):
        mark("col_wait")
        for k in range(1, n_col):
            j = lax.rem(mine + k, n_col)
            await_recv(buf.at[l, h, j], sem.at[l, h, j])
        mark("col_sum")
        summed = buf[l, h, 0].astype(F32)
        for j in range(1, n_col):
            summed = summed + buf[l, h, j].astype(F32)
        return (base.astype(F32) + (summed + bias.astype(F32))).astype(BF16)

    def project(l, h):
        mark("att_wait")
        for k in range(1, n_row):
            j = lax.rem(me + k, n_row)
            await_recv(att_in.at[l, h, j], att_sem.at[l, h, j])
        mark("wo_mm")
        gathered = att_in[l, h].reshape(n_row * head // 2, 2 * rows)
        both = [lax.dot_general(gathered, wo[l, i].reshape(n_row * head // 2, cols), (((0,), (0,)), ((), ())),
                                preferred_element_type=F32) for i in range(2)]
        proj_in[l, h, mine] = (both[0][0:rows] + both[1][rows:]).astype(BF16)
        col_send(proj_in, proj_sem, l, h)

    def up_go(l, h):
        n = 2 * l + 1
        mark("pair_wait")
        z, s1, s2 = normalize(n, h, ln2g, l)
        mark("up_mm")
        for i in range(n_chip):
            up_src[l, h, i] = jnp.dot(z, w1[l, i], preferred_element_type=F32).astype(BF16)
            if i < far:
                remote(up_src.at[l, h, i], up_in.at[l, h, i], send_sem.at[2], up_sem.at[l, h, i], {"row": peers[i]})
            if i == 0:
                send_stats(n, h, s1, s2)

    def up_recv(l, h):
        mark("up_wait")
        for i in range(far if h == 0 else 0):
            await_recv(cu_in.at[l, i], cu_sem.at[l, i])
        scales, shifts = stat_columns(2 * l + 1, h)
        total = jnp.zeros((rows, ff), F32)
        const = jnp.zeros((8, ff), F32)
        for i in (far, 1, 2, 0):
            if i < far:
                await_recv(up_in.at[l, h, i], up_sem.at[l, h, i])
            part = (up_in[l, h, i] if i < far else up_src[l, h, i]).astype(F32)
            side = cu_in[l, i] if i < far else cu_src[l, i]
            total = total + (part * scales[i] + shifts[i] * side[0:1])
            const = const + side
        mark("up_sum")
        own_at = pl.ds(pl.multiple_of(me * ff, ff), ff)
        bias = b1[l:l + 1, own_at].astype(F32)
        act_in[l, h, me] = jnp.maximum((total + const[1:2] + bias).astype(BF16), 0)
        for target in peers + [partner]:
            remote(act_in.at[l, h, me], act_in.at[l, h, me], send_sem.at[5], act_sem.at[l, h, me], {"row": target})

    def down(l, h):
        mark("act_wait")

        def term(j):
            return jnp.dot(act_in[l, h, j], w2[l, pl.ds(pl.multiple_of(j * ff, ff), ff), :], preferred_element_type=F32)

        part = term(me)
        await_recv(act_in.at[l, h, partner], act_sem.at[l, h, partner])
        part = part + term(partner)
        for j in arrivals:
            j = j + core
            await_recv(act_in.at[l, h, j], act_sem.at[l, h, j])
            remote(act_in.at[l, h, j], act_in.at[l, h, j], send_sem.at[5], act_sem.at[l, h, j], {"row": partner})
            part = part + term(j)
        mark("fwd_wait")
        for j in arrivals:
            j = j + 1 - core
            await_recv(act_in.at[l, h, j], act_sem.at[l, h, j])
            part = part + term(j)
        mark("down_mm")
        down_in[l, h, mine] = part.astype(BF16)
        col_send(down_in, down_sem, l, h)

    mark("side0")
    for i in range(4):
        await_recv(norms[i][1].at[1], pw_sem.at[0, 1 + n_chip + i])
    await_recv(w_in.at[0, cols:], pw_sem.at[0, 0])
    halves = range(HALVES)
    for l in range(layers):
        n = 2 * l
        for h in halves:
            qkv_go(l, h)
            if l == 0 and h == 0:
                qkv_side(0)
        if l == 0:
            share_up(0)
        for h in halves:
            qkv_recv(l, h)
            attend(l, h)
        mark("loads")
        if l + 1 < layers:
            loads["qkv", l + 1] = load_qkv(l + 1)
            load_cache(l + 1)
            loads["rest", l + 1] = load_rest(l + 1)
            share_up(l + 1)
        for copy in loads["rest", l]:
            copy.wait()
        for i in range(n_chip):
            await_recv(w1.at[l, i, cols:], pw_sem.at[l, 1 + i])
        up_side(l)
        for h in halves:
            project(l, h)
        if l + 1 < layers:
            mark("repack")
            for copy in loads["qkv", l + 1]:
                copy.wait()
            repack(l + 1)
            share_qkv(l + 1)
        for h in halves:
            state[n + 1, h] = col_recv(proj_in, proj_sem, l, h, bo[l:l + 1, :], state[n, h])
            swap_state(n + 1, h)
        for h in halves:
            up_go(l, h)
        if l + 1 < layers:
            mark("side")
            await_recv(w_in.at[l + 1, cols:], pw_sem.at[l + 1, 0])
            qkv_side(l + 1)
        for h in halves:
            up_recv(l, h)
        for h in halves:
            down(l, h)
        for h in halves:
            new_state = col_recv(down_in, down_sem, l, h, b2[l:l + 1, :], state[n + 1, h])
            if l + 1 < layers:
                state[n + 2, h] = new_state
                swap_state(n + 2, h)
            else:
                h_out[h * rows:(h + 1) * rows] = new_state
    mark("tail")
    for copy in pending:
        copy.wait_send()
    mark(None)


def store(*refs):
    copies = [pltpu.make_async_copy(refs[i], refs[3 + i], refs[6].at[i]) for i in range(3)]
    for copy in copies:
        copy.start()
    for copy in copies:
        copy.wait()


def solution(mesh):
    n_row = mesh.shape["row"]
    n_col = mesh.shape["col"]
    act_spec = P("dp", "row")
    cache_spec = P(None, "dp", ("col", "row"), None, None)
    fresh_spec = P(None, "dp", ("col", "row"), None)
    in_weight = P(None, "row", "col")
    out_weight = P(None, "col", "row")
    col_vec = P(None, "col")
    row_vec = P(None, "row")
    in_specs = (act_spec, P("dp"), cache_spec, cache_spec, row_vec, row_vec,
                in_weight, col_vec, in_weight, col_vec, in_weight, col_vec,
                out_weight, row_vec, row_vec, row_vec, in_weight, col_vec, out_weight, row_vec)

    def local_step(hidden, cache_len, k_cache, v_cache, *params):
        rows, cols = hidden.shape
        layers, _, _, s_max, head = k_cache.shape
        keys = jnp.swapaxes(k_cache, 3, 4).reshape(layers, rows, head, s_max)
        values = jnp.swapaxes(v_cache, 3, 4).reshape(layers, rows, head, s_max)
        operands = [hidden, cache_len.reshape(1, rows), keys, values, *params]
        operands[12] = params[8].reshape(layers, n_row, 2, head // 2, cols)
        dma = pltpu.SemaphoreType.DMA
        ff = params[12].shape[2]
        n_chip = n_row // 2
        ff_own = ff // n_row
        part = rows // HALVES
        shapes = [a.shape for a in operands]
        shapes = shapes[1:4] + [(2,) + s if i in (0, 1, 10, 11) else s for i, s in enumerate(shapes[4:])]
        shapes[11] = (layers, 2, n_row, head // 2, cols)
        shapes[15] = (layers, n_chip, 2 * cols, ff_own)
        vmem = [pltpu.VMEM(s, a.dtype) for s, a in zip(shapes, operands[1:])]
        scratch = vmem + [
            pltpu.VMEM((2 * layers, HALVES, part, cols), BF16),
            pltpu.VMEM((2 * layers, HALVES, part, cols), BF16),
            pltpu.VMEM((2 * layers, HALVES, 8, 128), F32),
            pltpu.VMEM((2 * layers, HALVES, n_chip - 1, 8, 128), F32),
            pltpu.VMEM((layers, n_chip, 8, 2 * head), F32),
            pltpu.VMEM((layers, n_chip - 1, 8, 2 * head), F32),
            pltpu.VMEM((layers, n_chip, 8, ff_own), F32),
            pltpu.VMEM((layers, n_chip - 1, 8, ff_own), F32),
            pltpu.VMEM((layers, 2 * cols, 3 * head * n_chip), BF16),
            pltpu.VMEM((layers, cols, 3 * head * n_chip), BF16),
            pltpu.VMEM((layers, HALVES, n_chip, part + part // 2, 2 * head), BF16),
            pltpu.VMEM((layers, HALVES, n_chip - 1, part + part // 2, 2 * head), BF16),
            pltpu.VMEM((layers, HALVES, n_row, head // 2, 2 * part), BF16),
            pltpu.VMEM((layers, HALVES, n_col, part, cols), BF16),
            pltpu.VMEM((layers, HALVES, n_chip, part, ff_own), BF16),
            pltpu.VMEM((layers, HALVES, n_chip - 1, part, ff_own), BF16),
            pltpu.VMEM((layers, HALVES, n_row, part, ff_own), BF16),
            pltpu.VMEM((layers, HALVES, n_col, part, cols), BF16),
            pltpu.VMEM((rows, 2 * head), BF16),
            pltpu.VMEM((16, 16 * head), BF16),
            pltpu.VMEM((rows, s_max), F32),
            pltpu.VMEM((HALVES, s_max, part), BF16),
            dma((1 + layers, 16)),
            dma((layers, 2, rows // 16)),
            dma((8,)),
            dma((layers, 5 + n_chip)),
            dma((2 * layers, HALVES)),
            dma((2 * layers, HALVES, n_chip - 1)),
            dma((layers, n_chip - 1)),
            dma((layers, n_chip - 1)),
            dma((layers, HALVES, n_chip - 1)),
            dma((layers, HALVES, n_row)),
            dma((layers, HALVES, n_col)),
            dma((layers, HALVES, n_chip - 1)),
            dma((layers, HALVES, n_row)),
            dma((layers, HALVES, n_col)),
        ]
        h, kt, vt = pl.pallas_call(
            functools.partial(kernel, n_row, n_col, cols * n_row),
            out_shape=(pltpu.VMEM((rows, cols), BF16),
                       pltpu.VMEM((layers, head, rows), BF16),
                       pltpu.VMEM((layers, head, rows), BF16)),
            in_specs=[pl.BlockSpec(memory_space=pltpu.HBM)] * len(operands),
            out_specs=[pl.BlockSpec(memory_space=pltpu.VMEM)] * 3,
            scratch_shapes=scratch,
            compiler_params=pltpu.CompilerParams(collective_id=0, has_side_effects=True,
                                                 vmem_limit_bytes=63 * 2 ** 20),
        )(*operands)
        h, kt, vt = pl.pallas_call(
            store,
            out_shape=(jax.ShapeDtypeStruct((rows, cols), BF16),
                       jax.ShapeDtypeStruct((layers, head, rows), BF16),
                       jax.ShapeDtypeStruct((layers, head, rows), BF16)),
            in_specs=[pl.BlockSpec(memory_space=pltpu.VMEM)] * 3,
            out_specs=[pl.BlockSpec(memory_space=pltpu.HBM)] * 3,
            scratch_shapes=[dma((3,))],
        )(*[pltpu.with_memory_space_constraint(a, pltpu.VMEM) for a in (h, kt, vt)])
        k_new = jnp.swapaxes(kt, 1, 2).reshape(layers, rows, 1, head)
        v_new = jnp.swapaxes(vt, 1, 2).reshape(layers, rows, 1, head)
        return h, k_new, v_new

    return jax.shard_map(local_step, mesh=mesh, in_specs=in_specs,
                         out_specs=(act_spec, fresh_spec, fresh_spec), check_vma=False)
```

time: 91.6 us -> 81.5 us (0.89)
  Pallas kernels: 90.9 us -> 80.8 us
    pallas_call x1, Pallas kernels: 90.2 us -> 80.1 us  [local_step(): pl.pallas_call(functools.partial(kernel, n_row, n_col, cols * n_row), out...]
where the time goes in v3:
time: 81.5 us; the launch traced here: 81.4 us
  Pallas kernels  80.8 us (99%)
    pallas_call x1, Pallas kernels, local_step(): pl.pallas_call(functools.partial(kernel, n_row, n_col, cols * n_row), out...  80.1 us

profile of v3, /device:TPU:97, one launch (start us, length us, event | category | flops | bytes accessed | tf_op | source)
XLA Modules:
  0.0 81.4 jit_solution(12942508296921312548)
XLA Ops:
  0.6 80.1 %shard_map.211 = (bf16[128,256]{1,0:T(8,128)(2,1)S(1)}, bf16[2,64,128]{2,1,0:T(8,128)(2,1)S(1)}, bf16[2,64,128]{2,1,0:T(8,128)(2,1)S(1)}) custom-call(bf16[128,256]{1,0:T(8,128)(2,1)} %x_hbm.1, s32[1,128]{1,0:T(1,128)} %bitcast.25, bf16[2,128,64,512]{3,2,1,0:T(8,128)(2,1)} %bitcast.22, bf16[2,128,64,512]{3,2,1,0:T(8,128)(2,1)} %bitcast.23, ...), custom_call_target="tpu_custom_call" | custom-call | tf_op jit(solution)/shard_map/pallas_call | solution.py:574
  80.7 0.7 shard_map.212

commit v4 on v0

v4 whole, which is shorter than its diff:
```python
import functools

import jax
import jax.numpy as jnp
from jax import lax
from jax.experimental import pallas as pl
from jax.experimental.pallas import tpu as pltpu
from jax.sharding import PartitionSpec as P

EPS_LN = 1e-5
F32 = jnp.float32
BF16 = jnp.bfloat16
MESH = pl.DeviceIdType.MESH


class Marks:
    def __init__(self):
        self.open = None

    def __call__(self, name):
        if self.open is not None:
            self.open.__exit__(None, None, None)
        self.open = None
        if name:
            self.open = jax.named_scope(name)
            self.open.__enter__()


HALVES = 2
STAGES = {"go": (0.6, 3.6), "attend": (3.1, 3.4), "project": (0.3, 3.6), "up": (0.6, 3.8), "act": (0.3, 3.7), "down": (0.4, 3.6)}


def stage_order(layers, parts):
    names = list(STAGES)
    ready = {part: 0.0 for part in range(parts)}
    done = {part: 0 for part in range(parts)}
    now, order = 0.0, []
    while ready:
        part = min(ready, key=lambda p: (max(ready[p], now), -done[p], p))
        if done[part] == layers * len(names):
            order.append(("end", layers, part))
            del ready[part]
            continue
        layer, name = divmod(done[part], len(names))
        cost, delay = STAGES[names[name]]
        now = max(now, ready[part]) + cost
        order.append((names[name], layer, part))
        done[part] += 1
        ready[part] = now + delay
    return order


def kernel(n_row, n_col, width,
           x_hbm, len_hbm, k_hbm, v_hbm, ln1g_hbm, ln1b_hbm, wq_hbm, bq_hbm, wk_hbm, bk_hbm, wv_hbm, bv_hbm,
           wo_hbm, bo_hbm, ln2g_hbm, ln2b_hbm, w1_hbm, b1_hbm, w2_hbm, b2_hbm,
           h_out, k_out, v_out,
           x_buf, len_buf, k_buf, v_buf, ln1g, ln1b, wq, bq, wk, bk, wv, bv, wo, bo, ln2g, ln2b, w1, b1, w2, b2,
           state, stat_src, stat_in, cq_src, cq_in, cu_src, cu_in, bias_own,
           qkv_src, qkv_in, att_src, att_in, proj_in, up_src, up_in, act_src, act_in, down_in, h_src, h_in, mid_in,
           twin, onehot, scores, probs_t,
           in_sem, kv_sem, send_sem, pw_sem, pair_sem, stat_sem, cq_sem, cu_sem,
           qkv_sem, att_sem, proj_sem, up_sem, act_sem, down_sem, h_sem, qw_sem):
    mark = Marks()
    mark("entry")
    layers = wo.shape[0]
    batch, cols = x_buf.shape
    rows = batch // HALVES
    sub = rows // 2
    head = k_buf.shape[2]
    s_max = k_buf.shape[3]
    lanes = 2 * head
    n_chip = n_row // 2
    near = 2 * cols
    ff = w1.shape[2] // n_row
    packs = 128 // sub
    thin = head // packs
    me = lax.axis_index("row")
    mine = lax.axis_index("col")
    chip = me // 2
    core = lax.rem(me, 2)
    partner = chip * 2 + (1 - core)
    flip = mine // 2
    side = lax.rem(core + flip, 2)
    hops = [2, 1, 3]
    far = len(hops)
    chips = [lax.rem(chip + dc, n_chip) for dc in hops] + [chip]
    mates = [c * 2 + core for c in chips[:far]]
    own_at = pl.ds(pl.multiple_of(core * cols, cols), cols)
    pending = []

    def local(src, dst, sem):
        copy = pltpu.make_async_copy(src, dst, sem)
        copy.start()
        return copy

    def remote(src, dst, ssem, rsem, target):
        copy = pltpu.make_async_remote_copy(src_ref=src, dst_ref=dst, send_sem=ssem, recv_sem=rsem,
                                            device_id=target, device_id_type=MESH)
        copy.start()
        pending.append(copy)

    def await_recv(dst, sem):
        pltpu.make_async_remote_copy(src_ref=dst, dst_ref=dst, send_sem=sem, recv_sem=sem,
                                     device_id={"row": me}, device_id_type=MESH).wait_recv()

    def everyone():
        for i in range(far):
            for e in (0, 1):
                yield i, e, chips[i] * 2 + lax.rem(e + flip, 2)
        yield far, 1 - side, partner

    def senders():
        for i in range(far):
            for e in (0, 1):
                yield i, e
        yield far, 1 - side

    def col_peer(k, half):
        y = lax.rem(mine + k, n_col)
        return {"row": chip * 2 + lax.rem(half + y // 2, 2), "col": y}

    def cache_copy(l, which, t):
        src, dst = ((k_hbm, k_buf), (v_hbm, v_buf))[which]
        return pltpu.make_async_copy(src.at[l, pl.ds(16 * t, 16)], dst.at[l, pl.ds(16 * t, 16)], kv_sem.at[l, which, t])

    shared = [(ln1g_hbm, ln1g), (ln1b_hbm, ln1b), (ln2g_hbm, ln2g), (ln2b_hbm, ln2b), (bo_hbm, bo), (b2_hbm, b2)]
    smalls = ([(x_hbm, x_buf), (len_hbm, len_buf), (bq_hbm, bq), (bk_hbm, bk), (bv_hbm, bv), (b1_hbm, b1)]
              + [(src, dst.at[core]) for src, dst in shared])
    small_copies = [local(src, dst, in_sem.at[0, i]) for i, (src, dst) in enumerate(smalls)]
    qkv_weights = [(wq_hbm, wq), (wk_hbm, wk), (wv_hbm, wv)]

    def load_qkv(l):
        return [local(src.at[l], dst.at[l, own_at], in_sem.at[1 + l, i]) for i, (src, dst) in enumerate(qkv_weights)]

    loads = {("qkv", 0): load_qkv(0)}
    barrier = pltpu.get_barrier_semaphore()
    for k in range(1, n_row):
        pl.semaphore_signal(barrier, inc=1, device_id={"row": lax.rem(me + k, n_row)}, device_id_type=MESH)
    for k in range(1, n_col):
        for e in (0, 1):
            pl.semaphore_signal(barrier, inc=1, device_id=col_peer(k, e), device_id_type=MESH)

    def rest_of(l):
        return ([(wo_hbm.at[l, :, i], wo.at[l, i, :, :, own_at]) for i in range(packs)]
                + [(w1_hbm.at[l], w1.at[l, own_at]), (w2_hbm.at[l], w2.at[l, :, own_at])])

    def load_rest(l):
        return [local(src, dst, in_sem.at[1 + l, 3 + i]) for i, (src, dst) in enumerate(rest_of(l))]

    def tile_at(i):
        return pl.ds(pl.multiple_of(chips[i] * lanes, lanes), lanes)

    def share_qkv(l):
        for i in range(n_chip):
            for t, (_, dst) in enumerate(qkv_weights):
                tile = dst.at[l, own_at, tile_at(i)]
                remote(tile, tile, send_sem.at[6], qw_sem.at[l, i, t], {"row": partner})

    def await_qkv(l, i):
        for t, (_, dst) in enumerate(qkv_weights):
            await_recv(dst.at[l, own_at, tile_at(i)], qw_sem.at[l, i, t])

    def share_rest(l, which):
        for i, (src, dst) in enumerate(rest_of(l)):
            if i in which:
                remote(src, dst, send_sem.at[7], pw_sem.at[l, 3 + i], {"row": partner})

    def await_rest(l, which):
        for i, (src, dst) in enumerate(rest_of(l)):
            if i in which:
                loads["rest", l][i].wait()
                await_recv(dst, pw_sem.at[l, 3 + i])

    ONLY_WO, ONLY_W1, ONLY_W2 = range(packs), (packs,), (packs + 1,)

    def load_cache(l):
        for which in range(2):
            for t in range(batch // 16):
                cache_copy(l, which, t).start()

    low = lax.broadcasted_iota(jnp.int32, (rows, lanes), 1) < head
    lane_id = lax.broadcasted_iota(jnp.int32, (16, 16 * head), 1)
    row_id = lax.broadcasted_iota(jnp.int32, (16, 16 * head), 0)
    onehot[...] = jnp.where(lane_id // head == row_id, 1.0, 0.0).astype(BF16)
    for copy in small_copies:
        copy.wait()

    def own_head(vec_ref, l):
        total = jnp.zeros((1, head), F32)
        for j in range(n_row):
            total = total + jnp.where(me == j, vec_ref[l:l + 1, j * head:(j + 1) * head].astype(F32), 0.0)
        return total

    zero = jnp.zeros((1, lanes), F32)
    for l in range(layers):
        vb = own_head(bv, l)
        bias_own[l] = jnp.concatenate([zero, jnp.concatenate([own_head(bq, l), own_head(bk, l)], axis=1), zero,
                                       jnp.concatenate([vb, vb], axis=1)] + [zero] * 4, axis=0)
    len_all = jnp.transpose(jnp.broadcast_to(len_buf[...], (batch, batch)))
    for h in range(HALVES):
        state[0, h, :, own_at] = x_buf[pl.ds(pl.multiple_of(h * rows + side * sub, sub), sub)]
    mark("load0")
    for copy in loads["qkv", 0]:
        copy.wait()
    load_cache(0)
    loads["rest", 0] = load_rest(0)
    for l in range(1, layers):
        loads["qkv", l] = load_qkv(l)
    mark("barrier")
    pl.semaphore_wait(barrier, n_row + 2 * n_col - 3)
    mark("entry2")
    for h in range(HALVES):
        there = pl.ds(pl.multiple_of(h * rows + (1 - side) * sub, sub), sub)
        remote(x_buf.at[there], state.at[0, h, :, own_at], send_sem.at[0], pair_sem.at[0, h], {"row": partner})
    for i, (src, dst) in enumerate(shared):
        remote(dst.at[core], dst.at[core], send_sem.at[6], pair_sem.at[1, i], {"row": partner})
    share_qkv(0)

    def full_row(ref, l):
        return jnp.concatenate([ref[0, l:l + 1], ref[1, l:l + 1]], axis=1).astype(F32)

    def side_operand(gain, shift, l):
        at = lax.broadcasted_iota(jnp.int32, (16, near), 0)
        return jnp.where(at == 0, full_row(gain, l), jnp.where(at == 1, full_row(shift, l), 0.0)).astype(BF16)

    def chip_tile(w, l, i):
        return w[l, :, tile_at(i)]

    def qkv_side(l):
        lhs = side_operand(ln1g, ln1b, l)
        for i in range(n_chip):
            q, k, v = [jnp.dot(lhs, chip_tile(w, l, i), preferred_element_type=F32)[0:8] for w in (wq, wk, wv)]
            q_r, k_r, v_r = [pltpu.roll(a, head, axis=1) for a in (q, k, v)]
            low8 = low[0:8]
            qk = jnp.where(core == 0, jnp.where(low8, q, k_r), jnp.where(low8, q_r, k))
            vs = jnp.where(core == 0, jnp.where(low8, v, v_r), jnp.where(low8, v_r, v))
            at = lax.broadcasted_iota(jnp.int32, (8, lanes), 0)
            cq_src[l, i] = jnp.where(at < 2, qk, pltpu.roll(vs, 2, axis=0))
        for i in range(far):
            remote(cq_src.at[l, i], cq_in.at[l, i], send_sem.at[1], cq_sem.at[l, i], {"row": mates[i]})

    def up_side(l):
        lhs = side_operand(ln2g, ln2b, l)
        for i in range(n_chip):
            at = pl.ds(pl.multiple_of((chips[i] * 2 + core) * ff, ff), ff)
            cu_src[l, i] = jnp.dot(lhs, w1[l, :, at], preferred_element_type=F32)[0:8]
        for i in range(far):
            remote(cu_src.at[l, i], cu_in.at[l, i], send_sem.at[1], cu_sem.at[l, i], {"row": mates[i]})

    def normalize(n, h, gain, l):
        mark("norm")
        x = state[n, h].astype(F32)
        s1 = jnp.sum(x, axis=1, keepdims=True)
        s2 = jnp.sum(x * x, axis=1, keepdims=True)
        mean = s1 / near
        inv = lax.rsqrt(jnp.maximum(s2 / near - mean * mean, 0.0) + EPS_LN)
        z = ((x - mean) * inv * full_row(gain, l)).astype(BF16)
        lane = lax.broadcasted_iota(jnp.int32, (sub, 128), 1)
        both = jnp.where(lane == 0, s1, jnp.where(lane == 1, s2, 0.0))
        both = jnp.concatenate([both, jnp.zeros((128 - sub, 128), F32)], axis=0)
        mine_stat = jnp.transpose(both)[0:2]
        stat_src[n, h] = mine_stat
        stat_in[n, h, far, side] = mine_stat
        return z

    def send_stats(n, h):
        for i, e, target in everyone():
            remote(stat_src.at[n, h], stat_in.at[n, h, i, side], send_sem.at[1], stat_sem.at[n, h, i, side], {"row": target})

    def stat_columns(n, h):
        for i, e in senders():
            await_recv(stat_in.at[n, h, i, e], stat_sem.at[n, h, i, e])
        table = []
        for e in (0, 1):
            parts = [stat_in[n, h, i, e] for i in range(n_chip)]
            total = parts[0]
            for part in parts[1:]:
                total = total + part
            mean = total[0:1] / width
            inv = lax.rsqrt(total[1:2] / width - mean * mean + EPS_LN)
            shifts = []
            for part in parts:
                near_mean = part[0:1] / near
                near_var = jnp.maximum(part[1:2] / near - near_mean * near_mean, 0.0) + EPS_LN
                table.append(inv * (near_var * lax.rsqrt(near_var)))
                shifts.append(inv * (near_mean - mean))
            table.extend(shifts)
        columns = jnp.concatenate(table + [jnp.zeros((128 - 4 * n_chip, 128), F32)], axis=0)
        columns = jnp.transpose(columns)[0:sub]

        def pick(start):
            return [[columns[:, e * 2 * n_chip + start + i:e * 2 * n_chip + start + i + 1] for i in range(n_chip)] for e in (0, 1)]

        return pick(0), pick(n_chip)

    def fold(column):
        return jnp.where(low[0:sub // 2], column[0:sub // 2], column[sub // 2:])

    def send_blocks(src, dst, sem, l, h, first, last):
        for i in range(first, last):
            for c in (0, 1) if i < far else (1 - core,):
                remote(src.at[l, h, i, c], dst.at[l, h, i, side], send_sem.at[2], sem.at[l, h, i, side],
                       {"row": chips[i] * 2 + c})
        if last == n_chip:
            dst[l, h, far, side] = src[l, h, far, core]

    fresh = {}

    def qkv_go(l, h):
        n = 2 * l
        z = normalize(n, h, ln1g, l)
        mark("qkv_mm")
        for i in range(n_chip):
            if l == 0 and h == 0:
                await_qkv(0, i)
            q, k, v = [jnp.dot(z, chip_tile(w, l, i), preferred_element_type=F32) for w in (wq, wk, wv)]
            q_r, k_r, v_r = [pltpu.roll(a, head, axis=1) for a in (q, k, v)]
            low_s, low_h = low[0:sub], low[0:sub // 2]
            qkv_src[l, h, i, 0, 0:sub] = jnp.where(low_s, q, k_r).astype(BF16)
            qkv_src[l, h, i, 1, 0:sub] = jnp.where(low_s, q_r, k).astype(BF16)
            qkv_src[l, h, i, 0, sub:] = jnp.where(low_h, v[:sub // 2], v_r[sub // 2:]).astype(BF16)
            qkv_src[l, h, i, 1, sub:] = jnp.where(low_h, v_r[:sub // 2], v[sub // 2:]).astype(BF16)
            if i == 0:
                send_blocks(qkv_src, qkv_in, qkv_sem, l, h, 0, 1)
                send_stats(n, h)
        send_blocks(qkv_src, qkv_in, qkv_sem, l, h, 1, n_chip)

    def qkv_recv(l, h):
        mark("qkv_wait")
        if h == 0:
            const = bias_own[l] + cq_src[l, far]
            cq_in[l, far] = cq_src[l, far]
            for i in range(far):
                await_recv(cq_in.at[l, i], cq_sem.at[l, i])
                const = const + cq_in[l, i]
            bias_own[l] = const
        scales, shifts = stat_columns(2 * l, h)
        qk, vv = [], []
        for e in (0, 1):
            a = jnp.broadcast_to(bias_own[l, 1:2], (sub, lanes))
            b = jnp.broadcast_to(bias_own[l, 3:4], (sub // 2, lanes))
            for i in range(n_chip):
                a = a + shifts[e][i] * cq_in[l, i, 0:1]
                b = b + fold(shifts[e][i]) * cq_in[l, i, 2:3]
            qk.append(a)
            vv.append(b)
        for i, e in senders():
            await_recv(qkv_in.at[l, h, i, e], qkv_sem.at[l, h, i, e])
        mark("qkv_sum")
        for e in (0, 1):
            for i in range(n_chip):
                qk[e] = qk[e] + qkv_in[l, h, i, e, 0:sub].astype(F32) * scales[e][i]
                vv[e] = vv[e] + qkv_in[l, h, i, e, sub:].astype(F32) * fold(scales[e][i])
        qk = jnp.concatenate(qk, axis=0)
        q_b = (qk[:, 0:head] * (head ** -0.5)).astype(BF16)
        k_new = pltpu.roll(qk, head, axis=1)[:, 0:head].astype(BF16)
        v_new = jnp.concatenate([piece for b in vv for piece in (b[:, 0:head], pltpu.roll(b, head, axis=1)[:, 0:head])],
                                axis=0).astype(BF16)
        q_f = q_b.astype(F32)
        k_f = k_new.astype(F32)
        twin[h * rows:(h + 1) * rows, :] = jnp.concatenate([q_f, q_f], axis=1).astype(BF16)
        fresh[l, h] = (jnp.sum(q_f * k_f, axis=1, keepdims=True), k_f, v_new.astype(F32))

    def attend(l, h):
        score_new, k_f, v_f = fresh[l, h]
        base = h * rows
        mine_rows = slice(base, base + rows)
        mark("scores")
        for t in range(rows // 16):
            cache_copy(l, 0, base // 16 + t).wait()
        for t in range(rows // 16):
            at = slice(base + 16 * t, base + 16 * (t + 1))
            q_diag = jnp.concatenate([twin[at, :]] * (16 * head // lanes), axis=1) * onehot[...]
            keys = k_buf[l, at].reshape(16 * head, s_max)
            scores[at, :] = jnp.dot(q_diag, keys, preferred_element_type=F32)
        mark("softmax")
        sc = scores[mine_rows, :]
        position = lax.broadcasted_iota(jnp.int32, sc.shape, 1)
        sc = jnp.where(position < len_all[mine_rows, 0:1], sc, -jnp.inf)
        peak = jnp.maximum(jnp.max(sc, axis=1, keepdims=True), score_new)
        ex = jnp.exp(sc - peak)
        ex_new = jnp.exp(score_new - peak)
        mass = jnp.sum(ex, axis=1, keepdims=True) + ex_new
        scores[mine_rows, :] = ex / mass
        prob_new = (ex_new / mass).astype(BF16).astype(F32)
        for b in range(s_max // 128):
            probs_t[h, b * 128:(b + 1) * 128, :] = jnp.transpose(scores[mine_rows, b * 128:(b + 1) * 128]).astype(BF16)
        prob_row = jnp.transpose(jnp.broadcast_to(prob_new, (rows, 128)))[0:1, :]
        lane = lax.broadcasted_iota(jnp.int32, (head, rows), 1)
        mark("mix")

        def mix_step(t, acc):
            for u in range(2):
                cache_copy(l, 1, base // 16 + 2 * t + u).wait()
            values = v_buf[l, pl.ds(base + 32 * t, 32)].reshape(32 * head, s_max)
            full = jnp.dot(values, probs_t[h], preferred_element_type=F32)
            for i in range(32):
                acc = jnp.where(lane == 32 * t + i, full[i * head:(i + 1) * head], acc)
            return acc

        mixed = lax.fori_loop(0, rows // 32, mix_step, jnp.zeros((head, rows), F32))
        mark("att_send")
        v_t = jnp.transpose(v_f)
        mixed = mixed + prob_row * v_t
        for e in (0, 1):
            att_src[l, h, e] = jnp.concatenate(
                [mixed[i * thin:(i + 1) * thin, e * sub:(e + 1) * sub] for i in range(packs)], axis=1).astype(BF16)
        for i, e, target in everyone():
            remote(att_src.at[l, h, e], att_in.at[l, h, me], send_sem.at[3], att_sem.at[l, h, me], {"row": target})
        att_in[l, h, me] = att_src[l, h, side]
        fresh[l, h] = (k_f, v_t)

    def keep_fresh(l, h):
        k_f, v_t = fresh[l, h]
        k_out[l, :, h * rows:(h + 1) * rows] = jnp.transpose(k_f).astype(BF16)
        v_out[l, :, h * rows:(h + 1) * rows] = v_t.astype(BF16)

    def col_send(buf, sem, l, h):
        mark("col_send")
        for k in (2, 1, 3):
            remote(buf.at[l, h, mine], buf.at[l, h, mine], send_sem.at[4], sem.at[l, h, mine], col_peer(k, side))

    def col_recv(buf, sem, l, h, bias, base):
        mark("col_wait")
        for k in range(1, n_col):
            j = lax.rem(mine + k, n_col)
            await_recv(buf.at[l, h, j], sem.at[l, h, j])
        mark("col_sum")
        summed = buf[l, h, 0].astype(F32)
        for j in range(1, n_col):
            summed = summed + buf[l, h, j].astype(F32)
        return (base.astype(F32) + (summed + full_row(bias, l))).astype(BF16)

    def project(l, h):
        mark("att_wait")
        for k in range(1, n_row):
            j = lax.rem(me + k, n_row)
            await_recv(att_in.at[l, h, j], att_sem.at[l, h, j])
        mark("wo_mm")
        gathered = att_in[l, h].reshape(n_row * thin, 128)
        total = jnp.zeros((sub, near), F32)
        for i in range(packs):
            total = total + lax.dot_general(gathered, wo[l, i].reshape(n_row * thin, near), (((0,), (0,)), ((), ())),
                                            preferred_element_type=F32)[i * sub:(i + 1) * sub]
        proj_in[l, h, mine] = total.astype(BF16)
        col_send(proj_in, proj_sem, l, h)

    def up_go(l, h):
        n = 2 * l + 1
        z = normalize(n, h, ln2g, l)
        mark("up_mm")
        for i in range(n_chip):
            at = pl.ds(pl.multiple_of(chips[i] * 2 * ff, 2 * ff), 2 * ff)
            full = jnp.dot(z, w1[l, :, at], preferred_element_type=F32).astype(BF16)
            for c in (0, 1):
                up_src[l, h, i, c] = full[:, c * ff:(c + 1) * ff]
            if i == 0:
                send_blocks(up_src, up_in, up_sem, l, h, 0, 1)
                send_stats(n, h)
        send_blocks(up_src, up_in, up_sem, l, h, 1, n_chip)

    def up_recv(l, h):
        mark("up_wait")
        if h == 0:
            const = b1[l:l + 1, pl.ds(pl.multiple_of(me * ff, ff), ff)].astype(F32) + cu_src[l, far, 1:2]
            cu_in[l, far] = cu_src[l, far]
            for i in range(far):
                await_recv(cu_in.at[l, i], cu_sem.at[l, i])
                const = const + cu_in[l, i, 1:2]
            cu_in[l, far, 1:2] = const
        scales, shifts = stat_columns(2 * l + 1, h)
        totals = []
        for e in (0, 1):
            total = jnp.broadcast_to(cu_in[l, far, 1:2], (sub, ff))
            for i in range(n_chip):
                total = total + shifts[e][i] * cu_in[l, i, 0:1]
            totals.append(total)
        for i, e in senders():
            await_recv(up_in.at[l, h, i, e], up_sem.at[l, h, i, e])
        mark("up_sum")
        for e in (0, 1):
            for i in range(n_chip):
                totals[e] = totals[e] + up_in[l, h, i, e].astype(F32) * scales[e][i]
            act_src[l, h, e] = jnp.maximum(totals[e].astype(BF16), 0)
        for i, e, target in everyone():
            remote(act_src.at[l, h, e], act_in.at[l, h, me], send_sem.at[5], act_sem.at[l, h, me], {"row": target})
        act_in[l, h, me] = act_src[l, h, side]

    def down(l, h):
        mark("act_wait")
        for k in range(1, n_row):
            j = lax.rem(me + k, n_row)
            await_recv(act_in.at[l, h, j], act_sem.at[l, h, j])
        mark("down_mm")
        both = jnp.concatenate([act_in[l, h, j] for j in range(n_row)], axis=1)
        part = jnp.dot(both, w2[l], preferred_element_type=F32).astype(BF16)
        if l + 1 < layers:
            down_in[l, h, mine] = part
            col_send(down_in, down_sem, l, h)
            return
        mark("col_send")
        for c in (0, 1):
            h_src[h, c] = part[:, c * cols:(c + 1) * cols]
        for k in (2, 1, 3):
            for c in (0, 1):
                remote(h_src.at[h, c], h_in.at[h, mine, side], send_sem.at[4], h_sem.at[h, mine, side],
                       {"row": chip * 2 + c, "col": lax.rem(mine + k, n_col)})
        remote(h_src.at[h, 1 - core], h_in.at[h, mine, side], send_sem.at[4], h_sem.at[h, mine, side], {"row": partner})
        h_in[h, mine, side] = h_src[h, core]

    def finish(h):
        mark("col_wait")
        await_recv(mid_in.at[h], pair_sem.at[2, h])
        for k in range(1, n_col):
            for e in (0, 1):
                j = lax.rem(mine + k, n_col)
                await_recv(h_in.at[h, j, e], h_sem.at[h, j, e])
        await_recv(h_in.at[h, mine, 1 - side], h_sem.at[h, mine, 1 - side])
        mark("last")
        bias = b2[core, layers - 1:layers].astype(F32)
        for e in (0, 1):
            summed = h_in[h, 0, e].astype(F32)
            for j in range(1, n_col):
                summed = summed + h_in[h, j, e].astype(F32)
            base = jnp.where(side == e, state[2 * layers - 1, h, :, own_at].astype(F32), mid_in[h].astype(F32))
            at = h * rows + e * sub
            h_out[at:at + sub] = (base + (summed + bias)).astype(BF16)

    mark("side0")
    for h in range(HALVES):
        await_recv(state.at[0, h, :, own_at], pair_sem.at[0, h])
    for i, (src, dst) in enumerate(shared):
        await_recv(dst.at[core], pair_sem.at[1, i])
    last = HALVES - 1
    for stage, l, h in stage_order(layers, HALVES):
        n = 2 * l
        if l > 0 and stage == "go":
            new_state = col_recv(down_in, down_sem, l - 1, h, b2, state[n - 1, h])
        if stage == "go":
            if l > 0:
                state[n, h] = new_state
            qkv_go(l, h)
            mark("side")
            if l == 0 and h == 0:
                qkv_side(0)
            if l == 0 and h == last:
                share_rest(0, range(packs + 2))
            if l > 0 and h == 0:
                await_rest(l, ONLY_W1)
                up_side(l)
        elif stage == "attend":
            qkv_recv(l, h)
            attend(l, h)
            if l + 1 < layers and h == 0:
                mark("side")
                for copy in loads["qkv", l + 1]:
                    copy.wait()
                share_qkv(l + 1)
                load_cache(l + 1)
                loads["rest", l + 1] = load_rest(l + 1)
                share_rest(l + 1, range(packs + 1))
            if l + 1 < layers and h == last:
                share_rest(l + 1, ONLY_W2)
        elif stage == "project":
            if h == 0:
                await_rest(l, ONLY_WO)
            project(l, h)
            mark("side")
            if h == 0 and l == 0:
                await_rest(l, ONLY_W1)
                up_side(l)
            keep_fresh(l, h)
        elif stage == "up":
            state[n + 1, h] = col_recv(proj_in, proj_sem, l, h, bo, state[n, h])
            up_go(l, h)
            if l + 1 == layers:
                there = pl.ds(pl.multiple_of((1 - core) * cols, cols), cols)
                remote(state.at[n + 1, h, :, there], mid_in.at[h], send_sem.at[0], pair_sem.at[2, h], {"row": partner})
            if h == 0 and l + 1 < layers:
                mark("side")
                for i in range(n_chip):
                    await_qkv(l + 1, i)
                qkv_side(l + 1)
        elif stage == "act":
            up_recv(l, h)
        elif stage == "down":
            if h == 0:
                await_rest(l, ONLY_W2)
            down(l, h)
        else:
            finish(h)
    mark("tail")
    for copy in pending:
        copy.wait_send()
    mark(None)


def store(*refs):
    copies = [pltpu.make_async_copy(refs[i], refs[3 + i], refs[6].at[i]) for i in range(3)]
    for copy in copies:
        copy.start()
    for copy in copies:
        copy.wait()


def solution(mesh):
    n_row = mesh.shape["row"]
    n_col = mesh.shape["col"]
    act_spec = P("dp", "row")
    cache_spec = P(None, "dp", ("col", "row"), None, None)
    fresh_spec = P(None, "dp", ("col", "row"), None)
    in_weight = P(None, "row", "col")
    out_weight = P(None, "col", "row")
    col_vec = P(None, "col")
    row_vec = P(None, "row")
    in_specs = (act_spec, P("dp"), cache_spec, cache_spec, row_vec, row_vec,
                in_weight, col_vec, in_weight, col_vec, in_weight, col_vec,
                out_weight, row_vec, row_vec, row_vec, in_weight, col_vec, out_weight, row_vec)

    def local_step(hidden, cache_len, k_cache, v_cache, *params):
        rows, cols = hidden.shape
        layers, _, _, s_max, head = k_cache.shape
        keys = jnp.swapaxes(k_cache, 3, 4).reshape(layers, rows, head, s_max)
        values = jnp.swapaxes(v_cache, 3, 4).reshape(layers, rows, head, s_max)
        operands = [hidden, cache_len.reshape(1, rows), keys, values, *params]
        packs = 256 * HALVES // rows
        operands[12] = params[8].reshape(layers, n_row, packs, head // packs, cols)
        dma = pltpu.SemaphoreType.DMA
        ff = params[12].shape[2]
        n_chip = n_row // 2
        ff_own = ff // n_row
        near = 2 * cols
        sub = rows // HALVES // 2
        shapes = [(2,) + a.shape if i in (4, 5, 13, 14, 15, 19) else a.shape for i, a in enumerate(operands)]
        for i in (6, 8, 10, 16):
            shapes[i] = (layers, near, shapes[i][2])
        shapes[12] = (layers, packs, n_row, head // packs, near)
        shapes[18] = (layers, ff, near)
        vmem = [pltpu.VMEM(s, a.dtype) for s, a in zip(shapes, operands)]
        block = sub + sub // 2
        scratch = vmem + [
            pltpu.VMEM((2 * layers, HALVES, sub, near), BF16),
            pltpu.VMEM((2 * layers, HALVES, 2, 128), F32),
            pltpu.VMEM((2 * layers, HALVES, n_chip, 2, 2, 128), F32),
            pltpu.VMEM((layers, n_chip, 8, 2 * head), F32),
            pltpu.VMEM((layers, n_chip, 8, 2 * head), F32),
            pltpu.VMEM((layers, n_chip, 8, ff_own), F32),
            pltpu.VMEM((layers, n_chip, 8, ff_own), F32),
            pltpu.VMEM((layers, 8, 2 * head), F32),
            pltpu.VMEM((layers, HALVES, n_chip, 2, block, 2 * head), BF16),
            pltpu.VMEM((layers, HALVES, n_chip, 2, block, 2 * head), BF16),
            pltpu.VMEM((layers, HALVES, 2, head // packs, 128), BF16),
            pltpu.VMEM((layers, HALVES, n_row, head // packs, 128), BF16),
            pltpu.VMEM((layers, HALVES, n_col, sub, near), BF16),
            pltpu.VMEM((layers, HALVES, n_chip, 2, sub, ff_own), BF16),
            pltpu.VMEM((layers, HALVES, n_chip, 2, sub, ff_own), BF16),
            pltpu.VMEM((layers, HALVES, 2, sub, ff_own), BF16),
            pltpu.VMEM((layers, HALVES, n_row, sub, ff_own), BF16),
            pltpu.VMEM((layers, HALVES, n_col, sub, near), BF16),
            pltpu.VMEM((HALVES, 2, sub, cols), BF16),
            pltpu.VMEM((HALVES, n_col, 2, sub, cols), BF16),
            pltpu.VMEM((HALVES, sub, cols), BF16),
            pltpu.VMEM((rows, 2 * head), BF16),
            pltpu.VMEM((16, 16 * head), BF16),
            pltpu.VMEM((rows, s_max), F32),
            pltpu.VMEM((HALVES, s_max, rows // HALVES), BF16),
            dma((1 + layers, 16)),
            dma((layers, 2, rows // 16)),
            dma((9,)),
            dma((layers, 5 + packs)),
            dma((3, 8)),
            dma((2 * layers, HALVES, n_chip, 2)),
            dma((layers, n_chip)),
            dma((layers, n_chip)),
            dma((layers, HALVES, n_chip, 2)),
            dma((layers, HALVES, n_row)),
            dma((layers, HALVES, n_col)),
            dma((layers, HALVES, n_chip, 2)),
            dma((layers, HALVES, n_row)),
            dma((layers, HALVES, n_col)),
            dma((HALVES, n_col, 2)),
            dma((layers, n_chip, 3)),
        ]
        h, kt, vt = pl.pallas_call(
            functools.partial(kernel, n_row, n_col, cols * n_row),
            out_shape=(pltpu.VMEM((rows, cols), BF16),
                       pltpu.VMEM((layers, head, rows), BF16),
                       pltpu.VMEM((layers, head, rows), BF16)),
            in_specs=[pl.BlockSpec(memory_space=pltpu.HBM)] * len(operands),
            out_specs=[pl.BlockSpec(memory_space=pltpu.VMEM)] * 3,
            scratch_shapes=scratch,
            compiler_params=pltpu.CompilerParams(collective_id=0, has_side_effects=True,
                                                 vmem_limit_bytes=63 * 2 ** 20),
        )(*operands)
        h, kt, vt = pl.pallas_call(
            store,
            out_shape=(jax.ShapeDtypeStruct((rows, cols), BF16),
                       jax.ShapeDtypeStruct((layers, head, rows), BF16),
                       jax.ShapeDtypeStruct((layers, head, rows), BF16)),
            in_specs=[pl.BlockSpec(memory_space=pltpu.VMEM)] * 3,
            out_specs=[pl.BlockSpec(memory_space=pltpu.HBM)] * 3,
            scratch_shapes=[dma((3,))],
        )(*[pltpu.with_memory_space_constraint(a, pltpu.VMEM) for a in (h, kt, vt)])
        k_new = jnp.swapaxes(kt, 1, 2).reshape(layers, rows, 1, head)
        v_new = jnp.swapaxes(vt, 1, 2).reshape(layers, rows, 1, head)
        return h, k_new, v_new

    return jax.shard_map(local_step, mesh=mesh, in_specs=in_specs,
                         out_specs=(act_spec, fresh_spec, fresh_spec), check_vma=False)
```

time: 557 us -> 73.8 us (0.13)
  waiting for transfers between devices: 388 us -> 0 us
  blocking collectives: 94.9 us -> 0 us
  Pallas kernels: 0 us -> 72.8 us
  matrix products: 40.1 us -> 0 us
  other arithmetic: 14.4 us -> 0 us
  between operations: 14.5 us -> 0.83 us
    psum x6 -> x0, waiting for transfers between devices: 255 us -> none  [the longest x2 103 us: local_step(): inner_sum = lax.psum(inner_part, 'row')]
    reduce_scatter x6 -> x0, waiting for transfers between devices: 132 us -> none  [head_projection(): summed = lax.psum_scatter(partial, 'row', scatter_dimension=1, tiled=True)]
    pallas_call x0 -> x2, Pallas kernels: none -> 72.8 us  [the longest x1 72.1 us: local_step(): pl.pallas_call(functools.partial(kernel, n_row, n_col, cols * n_row), out...]
    psum x4 -> x0, blocking collectives: 57.3 us -> none  [layer_norm(): stats = lax.psum(stats, 'row')]
    dot_general x16 -> x0, matrix products: 40.1 us -> none  [the longest x2 11.3 us: attention(): jnp.einsum('bhs,bhsd->bhd', prob_cache, v_layer, preferred_element_type=j...]
    all_gather x2 -> x0, blocking collectives: 37.6 us -> none  [local_step(): lax.all_gather(attended.reshape(batch_rows, heads_dev * head_dim), 'row',...]
  transfers between devices with their start and end apart: 12 -> 0, of which waited for: 12 -> 0; matrix products, arithmetic and copies ran while one was open for 7% -> 0% of each run, Pallas kernels for 0% -> 0%
where the time goes in v4:
time: 73.8 us; the launch traced here: 73.6 us
  Pallas kernels  72.8 us (99%)
  between operations  0.83 us (1%)
    pallas_call x1, Pallas kernels, local_step(): pl.pallas_call(functools.partial(kernel, n_row, n_col, cols * n_row), out...  72.1 us

profile of v4, /device:TPU:97, one launch (start us, length us, event | category | flops | bytes accessed | tf_op | source)
XLA Modules:
  0.0 73.6 jit_solution(14259860804503218734)
XLA Ops:
  0.6 72.1 %shard_map.211 = (bf16[128,256]{1,0:T(8,128)(2,1)S(1)}, bf16[2,64,128]{2,1,0:T(8,128)(2,1)S(1)}, bf16[2,64,128]{2,1,0:T(8,128)(2,1)S(1)}) custom-call(bf16[128,256]{1,0:T(8,128)(2,1)} %x_hbm.1, s32[1,128]{1,0:T(1,128)} %bitcast.25, bf16[2,128,64,512]{3,2,1,0:T(8,128)(2,1)} %bitcast.22, bf16[2,128,64,512]{3,2,1,0:T(8,128)(2,1)} %bitcast.23, ...), custom_call_target="tpu_custom_call" | custom-call | tf_op jit(solution)/shard_map/pallas_call | solution.py:684
  72.8 0.7 shard_map.212

commit v5 on v4

--- a/solution.py
+++ b/solution.py
@@ -10,7 +10,7 @@
 EPS_LN = 1e-5
 F32 = jnp.float32
 BF16 = jnp.bfloat16
-MESH = pl.DeviceIdType.MESH
+LOGICAL = pl.DeviceIdType.LOGICAL
 
 
 class Marks:
@@ -27,6 +27,7 @@
 
 
 HALVES = 2
+ON_VPU = 20
 STAGES = {"go": (0.6, 3.6), "attend": (3.1, 3.4), "project": (0.3, 3.6), "up": (0.6, 3.8), "act": (0.3, 3.7), "down": (0.4, 3.6)}
 
 
@@ -54,7 +55,7 @@
            x_hbm, len_hbm, k_hbm, v_hbm, ln1g_hbm, ln1b_hbm, wq_hbm, bq_hbm, wk_hbm, bk_hbm, wv_hbm, bv_hbm,
            wo_hbm, bo_hbm, ln2g_hbm, ln2b_hbm, w1_hbm, b1_hbm, w2_hbm, b2_hbm,
            h_out, k_out, v_out,
-           x_buf, len_buf, k_buf, v_buf, ln1g, ln1b, wq, bq, wk, bk, wv, bv, wo, bo, ln2g, ln2b, w1, b1, w2, b2,
+           x_buf, len_buf, k_buf, v_buf, ln1g, ln1b, wqkv, bq, bk, bv, wo, bo, ln2g, ln2b, w1, b1, w2, b2,
            state, stat_src, stat_in, cq_src, cq_in, cu_src, cu_in, bias_own,
            qkv_src, qkv_in, att_src, att_in, proj_in, up_src, up_in, act_src, act_in, down_in, h_src, h_in, mid_in,
            twin, onehot, scores, probs_t,
@@ -72,8 +73,7 @@
     n_chip = n_row // 2
     near = 2 * cols
     ff = w1.shape[2] // n_row
-    packs = 128 // sub
-    thin = head // packs
+    packs = 2
     me = lax.axis_index("row")
     mine = lax.axis_index("col")
     chip = me // 2
@@ -87,6 +87,8 @@
     mates = [c * 2 + core for c in chips[:far]]
     own_at = pl.ds(pl.multiple_of(core * cols, cols), cols)
     pending = []
+    line = (lax.axis_index("dp") * n_col + mine) * n_row
+    column = [(lax.axis_index("dp") * n_col + lax.rem(mine + k, n_col)) * n_row for k in range(n_col)]
 
     def local(src, dst, sem):
         copy = pltpu.make_async_copy(src, dst, sem)
@@ -95,13 +97,13 @@
 
     def remote(src, dst, ssem, rsem, target):
         copy = pltpu.make_async_remote_copy(src_ref=src, dst_ref=dst, send_sem=ssem, recv_sem=rsem,
-                                            device_id=target, device_id_type=MESH)
+                                            device_id=target, device_id_type=LOGICAL)
         copy.start()
         pending.append(copy)
 
     def await_recv(dst, sem):
         pltpu.make_async_remote_copy(src_ref=dst, dst_ref=dst, send_sem=sem, recv_sem=sem,
-                                     device_id={"row": me}, device_id_type=MESH).wait_recv()
+                                     device_id=line + me, device_id_type=LOGICAL).wait_recv()
 
     def everyone():
         for i in range(far):
@@ -117,7 +119,7 @@
 
     def col_peer(k, half):
         y = lax.rem(mine + k, n_col)
-        return {"row": chip * 2 + lax.rem(half + y // 2, 2), "col": y}
+        return column[k] + chip * 2 + lax.rem(half + y // 2, 2)
 
     def cache_copy(l, which, t):
         src, dst = ((k_hbm, k_buf), (v_hbm, v_buf))[which]
@@ -127,43 +129,44 @@
     smalls = ([(x_hbm, x_buf), (len_hbm, len_buf), (bq_hbm, bq), (bk_hbm, bk), (bv_hbm, bv), (b1_hbm, b1)]
               + [(src, dst.at[core]) for src, dst in shared])
     small_copies = [local(src, dst, in_sem.at[0, i]) for i, (src, dst) in enumerate(smalls)]
-    qkv_weights = [(wq_hbm, wq), (wk_hbm, wk), (wv_hbm, wv)]
 
     def load_qkv(l):
-        return [local(src.at[l], dst.at[l, own_at], in_sem.at[1 + l, i]) for i, (src, dst) in enumerate(qkv_weights)]
+        return [local(src.at[l, :, pl.ds(pl.multiple_of(chips[i] * lanes, lanes), lanes)],
+                      wqkv.at[l, own_at, (3 * i + t) * lanes:(3 * i + t + 1) * lanes],
+                      in_sem.at[1 + l, 3 * i + t]) for i in range(n_chip) for t, src in enumerate((wq_hbm, wk_hbm, wv_hbm))]
 
     loads = {("qkv", 0): load_qkv(0)}
     barrier = pltpu.get_barrier_semaphore()
     for k in range(1, n_row):
-        pl.semaphore_signal(barrier, inc=1, device_id={"row": lax.rem(me + k, n_row)}, device_id_type=MESH)
+        pl.semaphore_signal(barrier, inc=1, device_id=line + lax.rem(me + k, n_row), device_id_type=LOGICAL)
     for k in range(1, n_col):
         for e in (0, 1):
-            pl.semaphore_signal(barrier, inc=1, device_id=col_peer(k, e), device_id_type=MESH)
+            pl.semaphore_signal(barrier, inc=1, device_id=col_peer(k, e), device_id_type=LOGICAL)
 
     def rest_of(l):
-        return ([(wo_hbm.at[l, :, i], wo.at[l, i, :, :, own_at]) for i in range(packs)]
-                + [(w1_hbm.at[l], w1.at[l, own_at]), (w2_hbm.at[l], w2.at[l, :, own_at])])
+        return ([(wo_hbm.at[l], wo.at[l, :, i, :, own_at]) for i in range(packs)]
+                + [(w2_hbm.at[l], w2.at[l, :, own_at])]
+                + [(w1_hbm.at[l, :, pl.ds(pl.multiple_of(chips[i] * 2 * ff, 2 * ff), 2 * ff)],
+                    w1.at[l, own_at, i * 2 * ff:(i + 1) * 2 * ff]) for i in range(n_chip)])
 
     def load_rest(l):
-        return [local(src, dst, in_sem.at[1 + l, 3 + i]) for i, (src, dst) in enumerate(rest_of(l))]
+        return [local(src, dst, in_sem.at[1 + l, 3 * n_chip + i]) for i, (src, dst) in enumerate(rest_of(l))]
 
     def tile_at(i):
-        return pl.ds(pl.multiple_of(chips[i] * lanes, lanes), lanes)
+        return slice(i * 3 * lanes, (i + 1) * 3 * lanes)
 
     def share_qkv(l):
         for i in range(n_chip):
-            for t, (_, dst) in enumerate(qkv_weights):
-                tile = dst.at[l, own_at, tile_at(i)]
-                remote(tile, tile, send_sem.at[6], qw_sem.at[l, i, t], {"row": partner})
+            tile = wqkv.at[l, own_at, tile_at(i)]
+            remote(tile, tile, send_sem.at[6], qw_sem.at[l, i], line + partner)
 
     def await_qkv(l, i):
-        for t, (_, dst) in enumerate(qkv_weights):
-            await_recv(dst.at[l, own_at, tile_at(i)], qw_sem.at[l, i, t])
+        await_recv(wqkv.at[l, own_at, tile_at(i)], qw_sem.at[l, i])
 
     def share_rest(l, which):
         for i, (src, dst) in enumerate(rest_of(l)):
             if i in which:
-                remote(src, dst, send_sem.at[7], pw_sem.at[l, 3 + i], {"row": partner})
+                remote(src, dst, send_sem.at[7], pw_sem.at[l, 3 + i], line + partner)
 
     def await_rest(l, which):
         for i, (src, dst) in enumerate(rest_of(l)):
@@ -171,7 +174,7 @@
                 loads["rest", l][i].wait()
                 await_recv(dst, pw_sem.at[l, 3 + i])
 
-    ONLY_WO, ONLY_W1, ONLY_W2 = range(packs), (packs,), (packs + 1,)
+    ONLY_WO, ONLY_W2, ONLY_W1 = range(packs), (packs,), range(packs + 1, packs + 1 + n_chip)
 
     def load_cache(l):
         for which in range(2):
@@ -185,17 +188,6 @@
     for copy in small_copies:
         copy.wait()
 
-    def own_head(vec_ref, l):
-        total = jnp.zeros((1, head), F32)
-        for j in range(n_row):
-            total = total + jnp.where(me == j, vec_ref[l:l + 1, j * head:(j + 1) * head].astype(F32), 0.0)
-        return total
-
-    zero = jnp.zeros((1, lanes), F32)
-    for l in range(layers):
-        vb = own_head(bv, l)
-        bias_own[l] = jnp.concatenate([zero, jnp.concatenate([own_head(bq, l), own_head(bk, l)], axis=1), zero,
-                                       jnp.concatenate([vb, vb], axis=1)] + [zero] * 4, axis=0)
     len_all = jnp.transpose(jnp.broadcast_to(len_buf[...], (batch, batch)))
     for h in range(HALVES):
         state[0, h, :, own_at] = x_buf[pl.ds(pl.multiple_of(h * rows + side * sub, sub), sub)]
@@ -211,9 +203,9 @@
     mark("entry2")
     for h in range(HALVES):
         there = pl.ds(pl.multiple_of(h * rows + (1 - side) * sub, sub), sub)
-        remote(x_buf.at[there], state.at[0, h, :, own_at], send_sem.at[0], pair_sem.at[0, h], {"row": partner})
+        remote(x_buf.at[there], state.at[0, h, :, own_at], send_sem.at[0], pair_sem.at[0, h], line + partner)
     for i, (src, dst) in enumerate(shared):
-        remote(dst.at[core], dst.at[core], send_sem.at[6], pair_sem.at[1, i], {"row": partner})
+        remote(dst.at[core], dst.at[core], send_sem.at[6], pair_sem.at[1, i], line + partner)
     share_qkv(0)
 
     def full_row(ref, l):
@@ -223,13 +215,14 @@
         at = lax.broadcasted_iota(jnp.int32, (16, near), 0)
         return jnp.where(at == 0, full_row(gain, l), jnp.where(at == 1, full_row(shift, l), 0.0)).astype(BF16)
 
-    def chip_tile(w, l, i):
-        return w[l, :, tile_at(i)]
+    def qkv_tiles(lhs, l, first, last):
+        full = jnp.dot(lhs, wqkv[l, :, first * 3 * lanes:last * 3 * lanes], preferred_element_type=F32)
+        return [[full[:, (3 * i + t) * lanes:(3 * i + t + 1) * lanes] for t in range(3)] for i in range(last - first)]
 
     def qkv_side(l):
         lhs = side_operand(ln1g, ln1b, l)
-        for i in range(n_chip):
-            q, k, v = [jnp.dot(lhs, chip_tile(w, l, i), preferred_element_type=F32)[0:8] for w in (wq, wk, wv)]
+        for i, tiles in enumerate(qkv_tiles(lhs, l, 0, n_chip)):
+            q, k, v = [a[0:8] for a in tiles]
             q_r, k_r, v_r = [pltpu.roll(a, head, axis=1) for a in (q, k, v)]
             low8 = low[0:8]
             qk = jnp.where(core == 0, jnp.where(low8, q, k_r), jnp.where(low8, q_r, k))
@@ -237,15 +230,15 @@
             at = lax.broadcasted_iota(jnp.int32, (8, lanes), 0)
             cq_src[l, i] = jnp.where(at < 2, qk, pltpu.roll(vs, 2, axis=0))
         for i in range(far):
-            remote(cq_src.at[l, i], cq_in.at[l, i], send_sem.at[1], cq_sem.at[l, i], {"row": mates[i]})
+            remote(cq_src.at[l, i], cq_in.at[l, i], send_sem.at[1], cq_sem.at[l, i], line + mates[i])
 
     def up_side(l):
         lhs = side_operand(ln2g, ln2b, l)
         for i in range(n_chip):
-            at = pl.ds(pl.multiple_of((chips[i] * 2 + core) * ff, ff), ff)
+            at = pl.ds(pl.multiple_of((2 * i + core) * ff, ff), ff)
             cu_src[l, i] = jnp.dot(lhs, w1[l, :, at], preferred_element_type=F32)[0:8]
         for i in range(far):
-            remote(cu_src.at[l, i], cu_in.at[l, i], send_sem.at[1], cu_sem.at[l, i], {"row": mates[i]})
+            remote(cu_src.at[l, i], cu_in.at[l, i], send_sem.at[1], cu_sem.at[l, i], line + mates[i])
 
     def normalize(n, h, gain, l):
         mark("norm")
@@ -265,7 +258,7 @@
 
     def send_stats(n, h):
         for i, e, target in everyone():
-            remote(stat_src.at[n, h], stat_in.at[n, h, i, side], send_sem.at[1], stat_sem.at[n, h, i, side], {"row": target})
+            remote(stat_src.at[n, h], stat_in.at[n, h, i, side], send_sem.at[1], stat_sem.at[n, h, i, side], line + target)
 
     def stat_columns(n, h):
         for i, e in senders():
@@ -285,8 +278,7 @@
                 table.append(inv * (near_var * lax.rsqrt(near_var)))
                 shifts.append(inv * (near_mean - mean))
             table.extend(shifts)
-        columns = jnp.concatenate(table + [jnp.zeros((128 - 4 * n_chip, 128), F32)], axis=0)
-        columns = jnp.transpose(columns)[0:sub]
+        columns = jnp.transpose(jnp.concatenate(table, axis=0))[0:sub]
 
         def pick(start):
             return [[columns[:, e * 2 * n_chip + start + i:e * 2 * n_chip + start + i + 1] for i in range(n_chip)] for e in (0, 1)]
@@ -300,7 +292,7 @@
         for i in range(first, last):
             for c in (0, 1) if i < far else (1 - core,):
                 remote(src.at[l, h, i, c], dst.at[l, h, i, side], send_sem.at[2], sem.at[l, h, i, side],
-                       {"row": chips[i] * 2 + c})
+                       line + chips[i] * 2 + c)
         if last == n_chip:
             dst[l, h, far, side] = src[l, h, far, core]
 
@@ -309,11 +301,16 @@
     def qkv_go(l, h):
         n = 2 * l
         z = normalize(n, h, ln1g, l)
+        send_stats(n, h)
         mark("qkv_mm")
         for i in range(n_chip):
             if l == 0 and h == 0:
                 await_qkv(0, i)
-            q, k, v = [jnp.dot(z, chip_tile(w, l, i), preferred_element_type=F32) for w in (wq, wk, wv)]
+                q, k, v = qkv_tiles(z, l, i, i + 1)[0]
+            else:
+                if i < 2:
+                    tiles = qkv_tiles(z, l, i, 1 if i == 0 else n_chip)
+                q, k, v = tiles[max(i - 1, 0)]
             q_r, k_r, v_r = [pltpu.roll(a, head, axis=1) for a in (q, k, v)]
             low_s, low_h = low[0:sub], low[0:sub // 2]
             qkv_src[l, h, i, 0, 0:sub] = jnp.where(low_s, q, k_r).astype(BF16)
@@ -322,7 +319,6 @@
             qkv_src[l, h, i, 1, sub:] = jnp.where(low_h, v_r[:sub // 2], v[sub // 2:]).astype(BF16)
             if i == 0:
                 send_blocks(qkv_src, qkv_in, qkv_sem, l, h, 0, 1)
-                send_stats(n, h)
         send_blocks(qkv_src, qkv_in, qkv_sem, l, h, 1, n_chip)
 
     def qkv_recv(l, h):
@@ -381,39 +377,47 @@
         ex = jnp.exp(sc - peak)
         ex_new = jnp.exp(score_new - peak)
         mass = jnp.sum(ex, axis=1, keepdims=True) + ex_new
-        scores[mine_rows, :] = ex / mass
-        prob_new = (ex_new / mass).astype(BF16).astype(F32)
+        inv = 1.0 / mass
+        scores[mine_rows, :] = (ex * inv).astype(BF16).astype(F32)
+        prob_new = (ex_new * inv).astype(BF16).astype(F32)
         for b in range(s_max // 128):
             probs_t[h, b * 128:(b + 1) * 128, :] = jnp.transpose(scores[mine_rows, b * 128:(b + 1) * 128]).astype(BF16)
-        prob_row = jnp.transpose(jnp.broadcast_to(prob_new, (rows, 128)))[0:1, :]
         lane = lax.broadcasted_iota(jnp.int32, (head, rows), 1)
         mark("mix")
 
         def mix_step(t, acc):
             for u in range(2):
                 cache_copy(l, 1, base // 16 + 2 * t + u).wait()
-            values = v_buf[l, pl.ds(base + 32 * t, 32)].reshape(32 * head, s_max)
+            on_mxu = 32 - ON_VPU
+            values = v_buf[l, pl.ds(base + 32 * t, on_mxu)].reshape(on_mxu * head, s_max)
             full = jnp.dot(values, probs_t[h], preferred_element_type=F32)
-            for i in range(32):
+            for i in range(on_mxu, 32):
+                prob = scores[pl.ds(base + 32 * t + i, 1), :]
+                terms = v_buf[l, base + 32 * t + i].astype(F32) * prob
+                short = terms[:, 0:128]
+                for b in range(1, s_max // 128):
+                    short = short + terms[:, b * 128:(b + 1) * 128]
+                acc = jnp.where(lane == 32 * t + i, jnp.sum(short, axis=1, keepdims=True), acc)
+            for i in range(on_mxu):
                 acc = jnp.where(lane == 32 * t + i, full[i * head:(i + 1) * head], acc)
             return acc
 
         mixed = lax.fori_loop(0, rows // 32, mix_step, jnp.zeros((head, rows), F32))
         mark("att_send")
-        v_t = jnp.transpose(v_f)
-        mixed = mixed + prob_row * v_t
+        mixed = jnp.transpose(mixed) + prob_new * v_f
         for e in (0, 1):
-            att_src[l, h, e] = jnp.concatenate(
-                [mixed[i * thin:(i + 1) * thin, e * sub:(e + 1) * sub] for i in range(packs)], axis=1).astype(BF16)
+            first = mixed[e * sub:e * sub + sub // 2]
+            second = mixed[e * sub + sub // 2:(e + 1) * sub]
+            att_src[l, h, e] = jnp.concatenate([first, second], axis=1).astype(BF16)
         for i, e, target in everyone():
-            remote(att_src.at[l, h, e], att_in.at[l, h, me], send_sem.at[3], att_sem.at[l, h, me], {"row": target})
+            remote(att_src.at[l, h, e], att_in.at[l, h, me], send_sem.at[3], att_sem.at[l, h, me], line + target)
         att_in[l, h, me] = att_src[l, h, side]
-        fresh[l, h] = (k_f, v_t)
+        fresh[l, h] = (k_f, v_f)
 
     def keep_fresh(l, h):
-        k_f, v_t = fresh[l, h]
+        k_f, v_f = fresh[l, h]
         k_out[l, :, h * rows:(h + 1) * rows] = jnp.transpose(k_f).astype(BF16)
-        v_out[l, :, h * rows:(h + 1) * rows] = v_t.astype(BF16)
+        v_out[l, :, h * rows:(h + 1) * rows] = jnp.transpose(v_f).astype(BF16)
 
     def col_send(buf, sem, l, h):
         mark("col_send")
@@ -437,27 +441,28 @@
             j = lax.rem(me + k, n_row)
             await_recv(att_in.at[l, h, j], att_sem.at[l, h, j])
         mark("wo_mm")
-        gathered = att_in[l, h].reshape(n_row * thin, 128)
-        total = jnp.zeros((sub, near), F32)
-        for i in range(packs):
-            total = total + lax.dot_general(gathered, wo[l, i].reshape(n_row * thin, near), (((0,), (0,)), ((), ())),
-                                            preferred_element_type=F32)[i * sub:(i + 1) * sub]
+        low_h = low[0:sub // 2]
+        pieces = []
+        for j in range(n_row):
+            piece = att_in[l, h, j]
+            none = jnp.zeros_like(piece)
+            pieces.append(jnp.concatenate([jnp.where(low_h, piece, none), jnp.where(low_h, none, piece)], axis=0))
+        total = jnp.dot(jnp.concatenate(pieces, axis=1), wo[l].reshape(n_row * lanes, near), preferred_element_type=F32)
         proj_in[l, h, mine] = total.astype(BF16)
         col_send(proj_in, proj_sem, l, h)
 
     def up_go(l, h):
         n = 2 * l + 1
         z = normalize(n, h, ln2g, l)
+        send_stats(n, h)
         mark("up_mm")
-        for i in range(n_chip):
-            at = pl.ds(pl.multiple_of(chips[i] * 2 * ff, 2 * ff), 2 * ff)
-            full = jnp.dot(z, w1[l, :, at], preferred_element_type=F32).astype(BF16)
-            for c in (0, 1):
-                up_src[l, h, i, c] = full[:, c * ff:(c + 1) * ff]
-            if i == 0:
-                send_blocks(up_src, up_in, up_sem, l, h, 0, 1)
-                send_stats(n, h)
-        send_blocks(up_src, up_in, up_sem, l, h, 1, n_chip)
+        for first, last in ((0, 1), (1, n_chip)):
+            full = jnp.dot(z, w1[l, :, first * 2 * ff:last * 2 * ff], preferred_element_type=F32).astype(BF16)
+            for i in range(first, last):
+                for c in (0, 1):
+                    at = (2 * (i - first) + c) * ff
+                    up_src[l, h, i, c] = full[:, at:at + ff]
+            send_blocks(up_src, up_in, up_sem, l, h, first, last)
 
     def up_recv(l, h):
         mark("up_wait")
@@ -483,17 +488,25 @@
                 totals[e] = totals[e] + up_in[l, h, i, e].astype(F32) * scales[e][i]
             act_src[l, h, e] = jnp.maximum(totals[e].astype(BF16), 0)
         for i, e, target in everyone():
-            remote(act_src.at[l, h, e], act_in.at[l, h, me], send_sem.at[5], act_sem.at[l, h, me], {"row": target})
+            remote(act_src.at[l, h, e], act_in.at[l, h, me], send_sem.at[5], act_sem.at[l, h, me], line + target)
         act_in[l, h, me] = act_src[l, h, side]
 
     def down(l, h):
         mark("act_wait")
-        for k in range(1, n_row):
-            j = lax.rem(me + k, n_row)
-            await_recv(act_in.at[l, h, j], act_sem.at[l, h, j])
+        part = None
+        for place, dc in enumerate((0, 1, 3, 2)):
+            c = lax.rem(chip + n_chip - dc, n_chip)
+            if dc == 0:
+                await_recv(act_in.at[l, h, partner], act_sem.at[l, h, partner])
+            else:
+                for e in (0, 1):
+                    await_recv(act_in.at[l, h, 2 * c + e], act_sem.at[l, h, 2 * c + e])
+            both = jnp.concatenate([act_in[l, h, 2 * c], act_in[l, h, 2 * c + 1]], axis=1)
+            at = pl.ds(pl.multiple_of(c * 2 * ff, 2 * ff), 2 * ff)
+            term = jnp.dot(both, w2[l, at, :], preferred_element_type=F32)
+            part = term if part is None else part + term
         mark("down_mm")
-        both = jnp.concatenate([act_in[l, h, j] for j in range(n_row)], axis=1)
-        part = jnp.dot(both, w2[l], preferred_element_type=F32).astype(BF16)
+        part = part.astype(BF16)
         if l + 1 < layers:
             down_in[l, h, mine] = part
             col_send(down_in, down_sem, l, h)
@@ -504,8 +517,8 @@
         for k in (2, 1, 3):
             for c in (0, 1):
                 remote(h_src.at[h, c], h_in.at[h, mine, side], send_sem.at[4], h_sem.at[h, mine, side],
-                       {"row": chip * 2 + c, "col": lax.rem(mine + k, n_col)})
-        remote(h_src.at[h, 1 - core], h_in.at[h, mine, side], send_sem.at[4], h_sem.at[h, mine, side], {"row": partner})
+                       column[k] + chip * 2 + c)
+        remote(h_src.at[h, 1 - core], h_in.at[h, mine, side], send_sem.at[4], h_sem.at[h, mine, side], line + partner)
         h_in[h, mine, side] = h_src[h, core]
 
     def finish(h):
@@ -531,6 +544,19 @@
         await_recv(state.at[0, h, :, own_at], pair_sem.at[0, h])
     for i, (src, dst) in enumerate(shared):
         await_recv(dst.at[core], pair_sem.at[1, i])
+    def own_head(vec_ref, l):
+        total = jnp.zeros((1, head), F32)
+        for j in range(n_row):
+            total = total + jnp.where(me == j, vec_ref[l:l + 1, j * head:(j + 1) * head].astype(F32), 0.0)
+        return total
+
+    def own_biases():
+        zero = jnp.zeros((1, lanes), F32)
+        for l in range(layers):
+            vb = own_head(bv, l)
+            bias_own[l] = jnp.concatenate([zero, jnp.concatenate([own_head(bq, l), own_head(bk, l)], axis=1), zero,
+                                           jnp.concatenate([vb, vb], axis=1)] + [zero] * 4, axis=0)
+
     last = HALVES - 1
     for stage, l, h in stage_order(layers, HALVES):
         n = 2 * l
@@ -544,7 +570,10 @@
             if l == 0 and h == 0:
                 qkv_side(0)
             if l == 0 and h == last:
-                share_rest(0, range(packs + 2))
+                own_biases()
+                share_rest(0, ONLY_WO)
+                share_rest(0, ONLY_W1)
+                share_rest(0, ONLY_W2)
             if l > 0 and h == 0:
                 await_rest(l, ONLY_W1)
                 up_side(l)
@@ -558,7 +587,8 @@
                 share_qkv(l + 1)
                 load_cache(l + 1)
                 loads["rest", l + 1] = load_rest(l + 1)
-                share_rest(l + 1, range(packs + 1))
+                share_rest(l + 1, ONLY_WO)
+                share_rest(l + 1, ONLY_W1)
             if l + 1 < layers and h == last:
                 share_rest(l + 1, ONLY_W2)
         elif stage == "project":
@@ -575,7 +605,7 @@
             up_go(l, h)
             if l + 1 == layers:
                 there = pl.ds(pl.multiple_of((1 - core) * cols, cols), cols)
-                remote(state.at[n + 1, h, :, there], mid_in.at[h], send_sem.at[0], pair_sem.at[2, h], {"row": partner})
+                remote(state.at[n + 1, h, :, there], mid_in.at[h], send_sem.at[0], pair_sem.at[2, h], line + partner)
             if h == 0 and l + 1 < layers:
                 mark("side")
                 for i in range(n_chip):
@@ -623,8 +653,8 @@
         keys = jnp.swapaxes(k_cache, 3, 4).reshape(layers, rows, head, s_max)
         values = jnp.swapaxes(v_cache, 3, 4).reshape(layers, rows, head, s_max)
         operands = [hidden, cache_len.reshape(1, rows), keys, values, *params]
-        packs = 256 * HALVES // rows
-        operands[12] = params[8].reshape(layers, n_row, packs, head // packs, cols)
+        packs = 2
+        operands[12] = params[8].reshape(layers, n_row, head, cols)
         dma = pltpu.SemaphoreType.DMA
         ff = params[12].shape[2]
         n_chip = n_row // 2
@@ -632,11 +662,11 @@
         near = 2 * cols
         sub = rows // HALVES // 2
         shapes = [(2,) + a.shape if i in (4, 5, 13, 14, 15, 19) else a.shape for i, a in enumerate(operands)]
-        for i in (6, 8, 10, 16):
-            shapes[i] = (layers, near, shapes[i][2])
-        shapes[12] = (layers, packs, n_row, head // packs, near)
+        shapes[6] = (layers, near, 3 * shapes[6][2])
+        shapes[16] = (layers, near, ff)
+        shapes[12] = (layers, n_row, 2, head, near)
         shapes[18] = (layers, ff, near)
-        vmem = [pltpu.VMEM(s, a.dtype) for s, a in zip(shapes, operands)]
+        vmem = [pltpu.VMEM(s, a.dtype) for i, (s, a) in enumerate(zip(shapes, operands)) if i not in (8, 10)]
         block = sub + sub // 2
         scratch = vmem + [
             pltpu.VMEM((2 * layers, HALVES, sub, near), BF16),
@@ -649,8 +679,8 @@
             pltpu.VMEM((layers, 8, 2 * head), F32),
             pltpu.VMEM((layers, HALVES, n_chip, 2, block, 2 * head), BF16),
             pltpu.VMEM((layers, HALVES, n_chip, 2, block, 2 * head), BF16),
-            pltpu.VMEM((layers, HALVES, 2, head // packs, 128), BF16),
-            pltpu.VMEM((layers, HALVES, n_row, head // packs, 128), BF16),
+            pltpu.VMEM((layers, HALVES, 2, sub // 2, 2 * head), BF16),
+            pltpu.VMEM((layers, HALVES, n_row, sub // 2, 2 * head), BF16),
             pltpu.VMEM((layers, HALVES, n_col, sub, near), BF16),
             pltpu.VMEM((layers, HALVES, n_chip, 2, sub, ff_own), BF16),
             pltpu.VMEM((layers, HALVES, n_chip, 2, sub, ff_own), BF16),
@@ -664,10 +694,10 @@
             pltpu.VMEM((16, 16 * head), BF16),
             pltpu.VMEM((rows, s_max), F32),
             pltpu.VMEM((HALVES, s_max, rows // HALVES), BF16),
-            dma((1 + layers, 16)),
+            dma((1 + layers, 24)),
             dma((layers, 2, rows // 16)),
             dma((9,)),
-            dma((layers, 5 + packs)),
+            dma((layers, 5 + packs + n_chip)),
             dma((3, 8)),
             dma((2 * layers, HALVES, n_chip, 2)),
             dma((layers, n_chip)),
@@ -679,7 +709,7 @@
             dma((layers, HALVES, n_row)),
             dma((layers, HALVES, n_col)),
             dma((HALVES, n_col, 2)),
-            dma((layers, n_chip, 3)),
+            dma((layers, n_chip)),
         ]
         h, kt, vt = pl.pallas_call(
             functools.partial(kernel, n_row, n_col, cols * n_row),

time: 73.8 us -> 71.7 us (0.972)
  Pallas kernels: 72.8 us -> 70.7 us
    pallas_call x1, Pallas kernels: 72.1 us -> 70 us  [local_step(): pl.pallas_call(functools.partial(kernel, n_row, n_col, cols * n_row), out...]
where the time goes in v5:
time: 71.7 us; the launch traced here: 71.5 us
  Pallas kernels  70.7 us (99%)
  between operations  0.81 us (1%)
    pallas_call x1, Pallas kernels, local_step(): pl.pallas_call(functools.partial(kernel, n_row, n_col, cols * n_row), out...  70 us

profile of v5, /device:TPU:97, one launch (start us, length us, event | category | flops | bytes accessed | tf_op | source)
XLA Modules:
  0.0 71.5 jit_solution(8300000784624649322)
XLA Ops:
  0.6 70.0 %shard_map.211 = (bf16[128,256]{1,0:T(8,128)(2,1)S(1)}, bf16[2,64,128]{2,1,0:T(8,128)(2,1)S(1)}, bf16[2,64,128]{2,1,0:T(8,128)(2,1)S(1)}) custom-call(bf16[128,256]{1,0:T(8,128)(2,1)} %x_hbm.1, s32[1,128]{1,0:T(1,128)} %bitcast.25, bf16[2,128,64,512]{3,2,1,0:T(8,128)(2,1)} %bitcast.22, bf16[2,128,64,512]{3,2,1,0:T(8,128)(2,1)} %bitcast.23, ...), custom_call_target="tpu_custom_call" | custom-call | tf_op jit(solution)/shard_map/pallas_call | solution.py:714
  70.7 0.7 shard_map.212

commit v6 on v5

--- a/solution.py
+++ b/solution.py
@@ -27,6 +27,7 @@
 
 
 HALVES = 2
+SCORES_ON_VPU = 4
 ON_VPU = 20
 STAGES = {"go": (0.6, 3.6), "attend": (3.1, 3.4), "project": (0.3, 3.6), "up": (0.6, 3.8), "act": (0.3, 3.7), "down": (0.4, 3.6)}
 
@@ -157,8 +158,11 @@
 
     def share_qkv(l):
         for i in range(n_chip):
-            tile = wqkv.at[l, own_at, tile_at(i)]
-            remote(tile, tile, send_sem.at[6], qw_sem.at[l, i], line + partner)
+            share_tile(l, i)
+
+    def share_tile(l, i):
+        tile = wqkv.at[l, own_at, tile_at(i)]
+        remote(tile, tile, send_sem.at[6], qw_sem.at[l, i], line + partner)
 
     def await_qkv(l, i):
         await_recv(wqkv.at[l, own_at, tile_at(i)], qw_sem.at[l, i])
@@ -188,25 +192,31 @@
     for copy in small_copies:
         copy.wait()
 
-    len_all = jnp.transpose(jnp.broadcast_to(len_buf[...], (batch, batch)))
-    for h in range(HALVES):
-        state[0, h, :, own_at] = x_buf[pl.ds(pl.multiple_of(h * rows + side * sub, sub), sub)]
-    mark("load0")
-    for copy in loads["qkv", 0]:
-        copy.wait()
-    load_cache(0)
-    loads["rest", 0] = load_rest(0)
-    for l in range(1, layers):
-        loads["qkv", l] = load_qkv(l)
     mark("barrier")
     pl.semaphore_wait(barrier, n_row + 2 * n_col - 3)
     mark("entry2")
     for h in range(HALVES):
         there = pl.ds(pl.multiple_of(h * rows + (1 - side) * sub, sub), sub)
         remote(x_buf.at[there], state.at[0, h, :, own_at], send_sem.at[0], pair_sem.at[0, h], line + partner)
-    for i, (src, dst) in enumerate(shared):
-        remote(dst.at[core], dst.at[core], send_sem.at[6], pair_sem.at[1, i], line + partner)
-    share_qkv(0)
+
+    def share_vectors(which):
+        for i in which:
+            mine_half = shared[i][1].at[core]
+            remote(mine_half, mine_half, send_sem.at[6], pair_sem.at[1, i], line + partner)
+
+    share_vectors((0,))
+    for i in range(n_chip):
+        for t in range(3):
+            loads["qkv", 0][3 * i + t].wait()
+        share_tile(0, i)
+    share_vectors(range(1, len(shared)))
+    for h in range(HALVES):
+        state[0, h, :, own_at] = x_buf[pl.ds(pl.multiple_of(h * rows + side * sub, sub), sub)]
+    load_cache(0)
+    loads["rest", 0] = load_rest(0)
+    for l in range(1, layers):
+        loads["qkv", l] = load_qkv(l)
+    len_all = jnp.transpose(jnp.broadcast_to(len_buf[...], (batch, batch)))
 
     def full_row(ref, l):
         return jnp.concatenate([ref[0, l:l + 1], ref[1, l:l + 1]], axis=1).astype(F32)
@@ -364,11 +374,17 @@
         mark("scores")
         for t in range(rows // 16):
             cache_copy(l, 0, base // 16 + t).wait()
+        on_mxu = 16 - SCORES_ON_VPU
+        q_t = jnp.transpose(twin[mine_rows, :].astype(F32))[0:head]
         for t in range(rows // 16):
             at = slice(base + 16 * t, base + 16 * (t + 1))
-            q_diag = jnp.concatenate([twin[at, :]] * (16 * head // lanes), axis=1) * onehot[...]
-            keys = k_buf[l, at].reshape(16 * head, s_max)
-            scores[at, :] = jnp.dot(q_diag, keys, preferred_element_type=F32)
+            q_diag = jnp.concatenate([twin[at, :]] * (on_mxu * head // lanes), axis=1) * onehot[:, 0:on_mxu * head]
+            keys = k_buf[l, base + 16 * t:base + 16 * t + on_mxu].reshape(on_mxu * head, s_max)
+            scores[base + 16 * t:base + 16 * t + on_mxu, :] = jnp.dot(q_diag, keys, preferred_element_type=F32)[0:on_mxu]
+            for i in range(on_mxu, 16):
+                b = 16 * t + i
+                terms = k_buf[l, base + b].astype(F32) * q_t[:, b:b + 1]
+                scores[base + b:base + b + 1, :] = jnp.sum(terms, axis=0, keepdims=True)
         mark("softmax")
         sc = scores[mine_rows, :]
         position = lax.broadcasted_iota(jnp.int32, sc.shape, 1)
@@ -542,8 +558,7 @@
     mark("side0")
     for h in range(HALVES):
         await_recv(state.at[0, h, :, own_at], pair_sem.at[0, h])
-    for i, (src, dst) in enumerate(shared):
-        await_recv(dst.at[core], pair_sem.at[1, i])
+    await_recv(ln1g.at[core], pair_sem.at[1, 0])
     def own_head(vec_ref, l):
         total = jnp.zeros((1, head), F32)
         for j in range(n_row):
@@ -568,29 +583,28 @@
             qkv_go(l, h)
             mark("side")
             if l == 0 and h == 0:
+                for i in range(1, len(shared)):
+                    await_recv(shared[i][1].at[core], pair_sem.at[1, i])
                 qkv_side(0)
             if l == 0 and h == last:
                 own_biases()
                 share_rest(0, ONLY_WO)
                 share_rest(0, ONLY_W1)
                 share_rest(0, ONLY_W2)
+                for later in range(1, layers):
+                    load_cache(later)
+                    loads["rest", later] = load_rest(later)
             if l > 0 and h == 0:
                 await_rest(l, ONLY_W1)
                 up_side(l)
         elif stage == "attend":
             qkv_recv(l, h)
             attend(l, h)
-            if l + 1 < layers and h == 0:
+            if l + 1 < layers and h == last:
                 mark("side")
                 for copy in loads["qkv", l + 1]:
                     copy.wait()
                 share_qkv(l + 1)
-                load_cache(l + 1)
-                loads["rest", l + 1] = load_rest(l + 1)
-                share_rest(l + 1, ONLY_WO)
-                share_rest(l + 1, ONLY_W1)
-            if l + 1 < layers and h == last:
-                share_rest(l + 1, ONLY_W2)
         elif stage == "project":
             if h == 0:
                 await_rest(l, ONLY_WO)
@@ -599,10 +613,18 @@
             if h == 0 and l == 0:
                 await_rest(l, ONLY_W1)
                 up_side(l)
-            keep_fresh(l, h)
+            if h < last:
+                keep_fresh(l, h)
         elif stage == "up":
             state[n + 1, h] = col_recv(proj_in, proj_sem, l, h, bo, state[n, h])
             up_go(l, h)
+            if h == 0:
+                mark("side")
+                keep_fresh(l, last)
+                if l + 1 < layers:
+                    share_rest(l + 1, ONLY_WO)
+                    share_rest(l + 1, ONLY_W1)
+                    share_rest(l + 1, ONLY_W2)
             if l + 1 == layers:
                 there = pl.ds(pl.multiple_of((1 - core) * cols, cols), cols)
                 remote(state.at[n + 1, h, :, there], mid_in.at[h], send_sem.at[0], pair_sem.at[2, h], line + partner)

time: 71.7 us -> 71.2 us (level)
  no operation moved by 1% of the time
where the time goes in v6:
time: 71.2 us; the launch traced here: 71.1 us
  Pallas kernels  70.3 us (99%)
  between operations  0.81 us (1%)
    pallas_call x1, Pallas kernels, local_step(): pl.pallas_call(functools.partial(kernel, n_row, n_col, cols * n_row), out...  69.6 us

profile of v6, /device:TPU:97, one launch (start us, length us, event | category | flops | bytes accessed | tf_op | source)
XLA Modules:
  0.0 71.1 jit_solution(1081703999573685171)
XLA Ops:
  0.6 69.6 %shard_map.211 = (bf16[128,256]{1,0:T(8,128)(2,1)S(1)}, bf16[2,64,128]{2,1,0:T(8,128)(2,1)S(1)}, bf16[2,64,128]{2,1,0:T(8,128)(2,1)S(1)}) custom-call(bf16[128,256]{1,0:T(8,128)(2,1)} %x_hbm.1, s32[1,128]{1,0:T(1,128)} %bitcast.25, bf16[2,128,64,512]{3,2,1,0:T(8,128)(2,1)} %bitcast.22, bf16[2,128,64,512]{3,2,1,0:T(8,128)(2,1)} %bitcast.23, ...), custom_call_target="tpu_custom_call" | custom-call | tf_op jit(solution)/shard_map/pallas_call | solution.py:736
  70.3 0.7 shard_map.212

commit v7 on v6

--- a/solution.py
+++ b/solution.py
@@ -318,18 +318,18 @@
                 await_qkv(0, i)
                 q, k, v = qkv_tiles(z, l, i, i + 1)[0]
             else:
-                if i < 2:
-                    tiles = qkv_tiles(z, l, i, 1 if i == 0 else n_chip)
-                q, k, v = tiles[max(i - 1, 0)]
+                if i in (0, 2):
+                    tiles = qkv_tiles(z, l, i, i + 2)
+                q, k, v = tiles[i % 2]
             q_r, k_r, v_r = [pltpu.roll(a, head, axis=1) for a in (q, k, v)]
             low_s, low_h = low[0:sub], low[0:sub // 2]
             qkv_src[l, h, i, 0, 0:sub] = jnp.where(low_s, q, k_r).astype(BF16)
             qkv_src[l, h, i, 1, 0:sub] = jnp.where(low_s, q_r, k).astype(BF16)
             qkv_src[l, h, i, 0, sub:] = jnp.where(low_h, v[:sub // 2], v_r[sub // 2:]).astype(BF16)
             qkv_src[l, h, i, 1, sub:] = jnp.where(low_h, v_r[:sub // 2], v[sub // 2:]).astype(BF16)
-            if i == 0:
-                send_blocks(qkv_src, qkv_in, qkv_sem, l, h, 0, 1)
-        send_blocks(qkv_src, qkv_in, qkv_sem, l, h, 1, n_chip)
+            if i == 1:
+                send_blocks(qkv_src, qkv_in, qkv_sem, l, h, 0, 2)
+        send_blocks(qkv_src, qkv_in, qkv_sem, l, h, 2, n_chip)
 
     def qkv_recv(l, h):
         mark("qkv_wait")
@@ -472,7 +472,7 @@
         z = normalize(n, h, ln2g, l)
         send_stats(n, h)
         mark("up_mm")
-        for first, last in ((0, 1), (1, n_chip)):
+        for first, last in ((0, 2), (2, n_chip)):
             full = jnp.dot(z, w1[l, :, first * 2 * ff:last * 2 * ff], preferred_element_type=F32).astype(BF16)
             for i in range(first, last):
                 for c in (0, 1):

time: 71.2 us -> 70.7 us (level)
  no operation moved by 1% of the time
where the time goes in v7:
time: 70.7 us; the launch traced here: 70.6 us
  Pallas kernels  69.8 us (99%)
  between operations  0.81 us (1%)
    pallas_call x1, Pallas kernels, local_step(): pl.pallas_call(functools.partial(kernel, n_row, n_col, cols * n_row), out...  69.1 us

profile of v7, /device:TPU:97, one launch (start us, length us, event | category | flops | bytes accessed | tf_op | source)
XLA Modules:
  0.0 70.6 jit_solution(4484141611706682535)
XLA Ops:
  0.6 69.1 %shard_map.211 = (bf16[128,256]{1,0:T(8,128)(2,1)S(1)}, bf16[2,64,128]{2,1,0:T(8,128)(2,1)S(1)}, bf16[2,64,128]{2,1,0:T(8,128)(2,1)S(1)}) custom-call(bf16[128,256]{1,0:T(8,128)(2,1)} %x_hbm.1, s32[1,128]{1,0:T(1,128)} %bitcast.25, bf16[2,128,64,512]{3,2,1,0:T(8,128)(2,1)} %bitcast.22, bf16[2,128,64,512]{3,2,1,0:T(8,128)(2,1)} %bitcast.23, ...), custom_call_target="tpu_custom_call" | custom-call | tf_op jit(solution)/shard_map/pallas_call | solution.py:736
  69.8 0.7 shard_map.212
